TPU v7x, 32 devices: a whole 2x2x4 slice. The times are simulated.
32 devices in a mesh: row: 8 (over y, x, core), col: 4 (over z).
Axes of the slice: x: 2, y: 2, z: 4, core: 2. Of those that a mesh axis runs over, the one named last changes fastest.
Arguments:
- left_factors: float32 [128, 256, 32], P(None, ('row', 'col')), may hold values from -12 to 12
- right_factors: float32 [128, 128, 32], P(None, ('col', 'row')), may hold values from -12 to 12
- weight: float32 [1024, 128], replicated, may hold values from -0.1875 to 0.1875
- bias: float32 [128], replicated, may hold values from -2 to 2
- cotangent: float32 [256, 128, 128], P('row', 'col'), may hold values from -6 to 6
Outputs:
- pair_out: float32 [256, 128, 128], P('row', 'col')
- left_grad: float32 [128, 256, 32], P(None, ('row', 'col'))
- right_grad: float32 [128, 128, 32], P(None, ('col', 'row'))
- weight_grad: float32 [1024, 128], replicated
- bias_grad: float32 [128], replicated
All inputs are finite; a program needn't handle non-finite values.
Results may differ from a plain program's by a relative error of at most 0.0001.
Values sent between devices are 32-bit elements; how exact they have to be, the bound alone decides.
A program may use at most 64 MiB of HBM per device.

v0:
```python
import functools

import jax
import jax.numpy as jnp
from jax import lax
from jax.experimental import pallas as pl
from jax.experimental.pallas import tpu as pltpu
from jax.sharding import PartitionSpec as P

F32 = jnp.float32
BF16 = jnp.bfloat16
MESH = pl.DeviceIdType.MESH
VMEM = pl.BlockSpec(memory_space=pltpu.VMEM)
STEP = 8


def split(x):
    high = x.astype(BF16)
    return high, (x - high.astype(F32)).astype(BF16)


def dot(a, b):
    return lax.dot_general(a, b, (((1,), (0,)), ((), ())), preferred_element_type=F32)


def dot3(a_high, a_low, b_high, b_low):
    return dot(a_high, b_high) + (dot(a_high, b_low) + dot(a_low, b_high))


def dot_wide(a_high, a_low, b_both):
    half = b_both.shape[1] // 2
    wide = dot(a_high, b_both)
    return wide[:, 0:half] + (wide[:, half:] + dot(a_low, b_both[:, 0:half]))


def swap_groups(pieces):
    lane = lax.broadcasted_iota(jnp.int32, pieces[0].shape, 1)
    low = lane < 64
    even = (lane & 32) == 0

    def far(a, b):
        moved = pltpu.roll(jnp.where(low, b, a), 64, 1)
        return jnp.where(low, a, moved), jnp.where(low, moved, b)

    def near(a, b):
        return (
            jnp.where(even, a, pltpu.roll(b, 32, 1)),
            jnp.where(even, pltpu.roll(a, 96, 1), b),
        )

    p0, p2 = far(pieces[0], pieces[2])
    p1, p3 = far(pieces[1], pieces[3])
    p0, p1 = near(p0, p1)
    p2, p3 = near(p2, p3)
    return p0, p1, p2, p3


def tile_kernel(
    nrow, ncol, width, l_ref, r_ref, w_ref, b_ref, cot_ref,
    pair_ref, lg_ref, rg_ref, wg_ref, bg_ref,
    lo, ro, lp, lbuf, rp, rbuf, wp, wbuf, part,
    l_c, l_l, lt_c, r_h, r_l, rt_c, w_c, wt_h, wt_l,
    c_h, c_l, ct_h, ct_l, h_h, h_l, o_scr, t_h, t_l, tmp,
    gls, glr, grs, grr, ls, lr, rs, rr, ws, wr, vs, vr, us, ur, xs, xr, fs, fr,
):
    row, col = lax.axis_index("row"), lax.axis_index("col")
    lw, samples = l_ref.shape
    rw = r_ref.shape[0]
    tile_rows, tile_cols = ncol * lw // width, nrow * rw // width
    channels, pair_width = w_ref.shape
    scale = 1.0 / samples
    per = 128 // width
    chunk = channels // nrow
    share = channels // (nrow * ncol)

    def in_row(peer):
        return {"row": peer, "col": col}

    def in_col(peer):
        return {"row": row, "col": peer}

    def block(ref, index, size):
        return ref.at[pl.ds(pl.multiple_of(index * size, size), size)]

    def each(count, here, act):
        @pl.loop(1, count)
        def _(k):
            act(lax.rem(here + k, count))

    def send(src, dst, send_sem, recv_sem, device):
        return pltpu.make_async_remote_copy(
            src_ref=src, dst_ref=dst, send_sem=send_sem, recv_sem=recv_sem,
            device_id=device, device_id_type=MESH,
        )

    def left_gather(peer, slot):
        return send(l_ref, block(lo, slot, lw), gls.at[peer], glr.at[slot], in_col(peer))

    def right_gather(peer, slot):
        return send(r_ref, block(ro, slot, rw), grs.at[peer], grr.at[slot], in_row(peer))

    def left_term(peer, slot):
        return send(block(lp, peer, lw), lbuf.at[slot], ls.at[peer], lr.at[slot], in_col(peer))

    def right_term(peer, slot):
        return send(block(rp, peer, rw), rbuf.at[slot], rs.at[peer], rr.at[slot], in_row(peer))

    def weight_row_term(peer, slot):
        return send(wp.at[peer], wbuf.at[slot], ws.at[peer], wr.at[slot], in_row(peer))

    def weight_col_term(peer, slot):
        return send(part.at[0, peer], part.at[1, slot], vs.at[peer], vr.at[slot], in_col(peer))

    def weight_col_whole(peer, slot):
        return send(wg_ref.at[row, col], wg_ref.at[row, slot], us.at[peer], ur.at[slot], in_col(peer))

    def weight_row_whole(peer, slot):
        return send(wg_ref.at[row], wg_ref.at[slot], xs.at[peer], xr.at[slot], in_row(peer))

    partner = row + 1 - 2 * lax.rem(row, 2)

    def weight_pass(index):
        return send(wg_ref.at[index], wg_ref.at[index], fs.at[index], fr.at[index], in_row(partner))

    def same_core(act):
        @pl.loop(1, nrow // 2)
        def _(k):
            act(lax.rem(row + 2 * k, nrow))

    barrier = pltpu.get_barrier_semaphore()
    each(ncol, col, lambda p: pl.semaphore_signal(
        barrier, inc=1, device_id=in_col(p), device_id_type=MESH))
    each(nrow, row, lambda p: pl.semaphore_signal(
        barrier, inc=1, device_id=in_row(p), device_id_type=MESH))
    pl.semaphore_wait(barrier, nrow + ncol - 2)
    each(ncol, col, lambda p: left_gather(p, col).start())
    each(nrow, row, lambda p: right_gather(p, row).start())

    for d in range(width):
        tmp[d * width : (d + 1) * width, :] = w_ref[pl.ds(d, width, stride=width), :]
    weight = tmp[0:channels, :]
    w_c[:, 0:pair_width], w_c[:, pair_width:] = split(weight)
    wt_h[...], wt_l[...] = split(weight.T)
    cot = cot_ref[...]
    c_h[...], c_l[...] = split(cot)
    ct_h[...], ct_l[...] = split(cot.T)
    bias_tail = jnp.broadcast_to(jnp.sum(cot, axis=0, keepdims=True), (8, pair_width))
    pair_ref[...] = jnp.broadcast_to(b_ref[...], pair_ref.shape)

    step_lanes, step_rows = STEP * width, STEP * tile_cols
    halves = step_lanes // 128

    @pl.loop(0, tile_rows // STEP)
    def _(g):
        rows = pl.ds(pl.multiple_of(g * step_rows, step_rows), step_rows)
        grad = dot3(c_h[rows, :], c_l[rows, :], wt_h[...], wt_l[...]) * scale
        for b in range(width // per):
            for half in range(halves):
                pieces = [
                    grad[(half * per + a) * tile_cols : (half * per + a + 1) * tile_cols,
                         b * 128 : (b + 1) * 128]
                    for a in range(per)
                ]
                lanes = pl.ds(pl.multiple_of(g * step_lanes + half * 128, 128), 128)
                for a, piece in enumerate(swap_groups(pieces)):
                    at = (b * per + a) * tile_cols
                    high, low = split(piece)
                    h_h[at : at + tile_cols, lanes] = high
                    h_l[at : at + tile_cols, lanes] = low

    ro[pl.ds(pl.multiple_of(row * rw, rw), rw), :] = r_ref[...]
    each(nrow, row, lambda p: right_gather(p, p).wait())
    for d in range(width):
        tmp[d * tile_cols : (d + 1) * tile_cols, :] = ro[pl.ds(d, tile_cols, stride=width), :]
    right = tmp[0 : width * tile_cols, :]
    rt_c[:, 0:samples], rt_c[:, samples:] = split(right)
    r_h[...], r_l[...] = split(right.T)
    lo[pl.ds(pl.multiple_of(col * lw, lw), lw), :] = l_ref[...]
    each(ncol, col, lambda p: left_gather(p, p).wait())

    @pl.loop(0, tile_rows // STEP)
    def _(g):
        lanes = pl.ds(pl.multiple_of(g * step_lanes, step_lanes), step_lanes)
        lp[lanes, :] = dot3(r_h[...], r_l[...], h_h[:, lanes], h_l[:, lanes]).T

    each(ncol, col, lambda p: left_term(p, col).start())
    lbuf[col] = lp[pl.ds(pl.multiple_of(col * lw, lw), lw), :]
    left = lo[...]
    lt_c[:, 0:samples], lt_c[:, samples:] = split(left)
    high, l_l[...] = split(left.T)
    l_c[0:samples, :] = high
    l_c[samples:, :] = high

    blocks = width // STEP
    block_rows, block_cols = STEP * tile_cols, STEP * width
    chunks = block_cols // chunk

    @pl.loop(0, blocks)
    def _(k):
        b = lax.rem(row // chunks + 1 + k, blocks)
        rows = pl.ds(pl.multiple_of(b * block_rows, block_rows), block_rows)
        cols = pl.ds(pl.multiple_of(b * block_cols, block_cols), block_cols)
        o_scr[...] = (
            dot(rt_c[rows, :], l_c[...]) + dot(rt_c[rows, 0:samples], l_l[...])
        ) * scale
        for q in range(STEP // per):
            for i in range(tile_rows // per):
                pieces = [
                    o_scr[(q * per + a) * tile_cols : (q * per + a + 1) * tile_cols,
                          i * 128 : (i + 1) * 128]
                    for a in range(per)
                ]
                for a, piece in enumerate(swap_groups(pieces)):
                    at = (i * per + a) * tile_cols
                    high, low = split(piece)
                    t_h[at : at + tile_cols, q * 128 : (q + 1) * 128] = high
                    t_l[at : at + tile_cols, q * 128 : (q + 1) * 128] = low
        terms = dot3(ct_h[...], ct_l[...], t_h[...], t_l[...]).T
        for m in range(chunks):
            peer = b * chunks + m
            wp[peer, 0:chunk, :] = terms[m * chunk : (m + 1) * chunk, :]
            wp[peer, chunk : chunk + 8, :] = bias_tail

            @pl.when(peer != row)
            def _():
                weight_row_term(peer, row).start()

        pair_ref[...] += dot_wide(t_h[...], t_l[...], w_c[cols, :])

    for d in range(width):
        rows = slice(d * tile_cols, (d + 1) * tile_cols)
        rp[pl.ds(d, tile_cols, stride=width), :] = dot_wide(h_h[rows, :], h_l[rows, :], lt_c[...])
    each(nrow, row, lambda p: weight_row_term(p, p).wait())
    wbuf[row] = wp[row]
    total = functools.reduce(lambda a, b: a + b, [wbuf[q] for q in range(nrow)])
    for q in range(ncol):
        part[0, q, 0:share, :] = total[q * share : (q + 1) * share, :]
        part[0, q, share : share + 8, :] = total[chunk : chunk + 8, :]
    each(ncol, col, lambda p: weight_col_term(p, col).start())
    each(nrow, row, lambda p: right_term(p, row).start())
    rbuf[row] = rp[pl.ds(pl.multiple_of(row * rw, rw), rw), :]
    part[1, col] = part[0, col]
    each(ncol, col, lambda p: weight_col_term(p, p).wait())
    total = functools.reduce(lambda a, b: a + b, [part[1, q] for q in range(ncol)])
    total = total / (tile_rows * nrow)
    wg_ref[row, col] = total[0:share, :]
    bg_ref[...] = total[share : share + 1, :]
    each(ncol, col, lambda p: weight_col_whole(p, col).start())
    each(ncol, col, lambda p: left_term(p, p).wait())
    lg_ref[...] = functools.reduce(lambda a, b: a + b, [lbuf[q] for q in range(ncol)])
    each(ncol, col, lambda p: weight_col_whole(p, p).wait())
    weight_pass(row).start()
    same_core(lambda p: weight_row_whole(p, row).start())

    def pass_on(p):
        weight_row_whole(p, p).wait_recv()
        weight_pass(p).start()

    same_core(pass_on)
    each(nrow, row, lambda p: right_term(p, p).wait())
    rg_ref[...] = functools.reduce(lambda a, b: a + b, [rbuf[q] for q in range(nrow)])
    same_core(lambda p: weight_row_whole(p, p).wait_send())

    @pl.loop(0, nrow // 2)
    def _(k):
        weight_pass(lax.rem(row + 2 * k, nrow)).wait_send()
        weight_pass(lax.rem(partner + 2 * k, nrow)).wait_recv()


def finish_kernel(
    width, pair_ref, lg_ref, rg_ref, wg_ref, bg_ref,
    pair_out, lg_out, rg_out, w_out, bg_out, held, sems,
):
    copies = [
        pltpu.make_async_copy(src, dst, sems.at[k])
        for k, (src, dst) in enumerate([
            (wg_ref, held), (pair_ref, pair_out), (lg_ref, lg_out), (rg_ref, rg_out), (bg_ref, bg_out),
        ])
    ]
    for copy in copies:
        copy.start()
    copies[0].wait()
    nrow, ncol, share, _ = held.shape
    for r in range(nrow):
        for q in range(ncol):
            d, c = divmod((r * ncol + q) * share, width)
            w_out[pl.ds(c * width + d, share, stride=width), :] = held[r, q]
    for copy in copies[1:]:
        copy.wait()


def per_device(nrow, ncol, left_factors, right_factors, weight, bias, cotangent):
    samples, li, width = left_factors.shape
    rj = right_factors.shape[1]
    tile_rows, tile_cols, pair_width = cotangent.shape
    channels = weight.shape[0]
    lw, rw = li * width, rj * width
    lefts, rights = tile_rows * width, tile_cols * width
    chunk, share = channels // nrow, channels // (nrow * ncol)
    dma = pltpu.SemaphoreType.DMA

    def shape(*dims):
        return jax.ShapeDtypeStruct(dims, F32)

    def two(*dims):
        return [pltpu.VMEM(dims, BF16)] * 2

    def buf(*dims):
        return pltpu.VMEM(dims, F32)

    scratch = [
        buf(lefts, samples), buf(rights, samples),
        buf(lefts, samples), buf(ncol, lw, samples),
        buf(rights, samples), buf(nrow, rw, samples),
        buf(nrow, chunk + 8, pair_width), buf(nrow, chunk + 8, pair_width),
        buf(2, ncol, share + 8, pair_width),
        pltpu.VMEM((2 * samples, lefts), BF16), pltpu.VMEM((samples, lefts), BF16),
        pltpu.VMEM((lefts, 2 * samples), BF16),
        *two(samples, rights), pltpu.VMEM((rights, 2 * samples), BF16),
        pltpu.VMEM((channels, 2 * pair_width), BF16), *two(pair_width, channels),
        *two(tile_rows * tile_cols, pair_width), *two(pair_width, tile_rows * tile_cols),
        *two(rights, lefts),
        buf(STEP * tile_cols, lefts), *two(tile_rows * tile_cols, STEP * width),
        buf(max(rights, channels), 128),
    ]
    for count in (ncol, nrow, ncol, nrow, nrow, ncol, ncol, nrow, nrow):
        scratch += [dma((count,)), dma((count,))]
    pair, lg, rg, wg, bg = pl.pallas_call(
        functools.partial(tile_kernel, nrow, ncol, width),
        out_shape=(
            shape(tile_rows * tile_cols, pair_width), shape(lw, samples), shape(rw, samples),
            shape(nrow, ncol, share, pair_width), shape(1, pair_width),
        ),
        in_specs=[VMEM] * 5,
        out_specs=[VMEM] * 5,
        scratch_shapes=scratch,
        compiler_params=pltpu.CompilerParams(collective_id=0, has_side_effects=True),
        name="tile",
    )(
        left_factors.transpose(1, 2, 0).reshape(lw, samples),
        right_factors.transpose(1, 2, 0).reshape(rw, samples),
        weight,
        bias.reshape(1, pair_width),
        cotangent.reshape(tile_rows * tile_cols, pair_width),
    )
    whole = pl.BlockSpec(memory_space=pl.ANY)
    pair, lg, rg, wg, bg = pl.pallas_call(
        functools.partial(finish_kernel, width),
        out_shape=(
            shape(tile_rows * tile_cols, pair_width), shape(lw, samples), shape(rw, samples),
            shape(channels, pair_width), shape(1, pair_width),
        ),
        in_specs=[whole] * 5,
        out_specs=[VMEM] * 5,
        scratch_shapes=[buf(nrow, ncol, share, pair_width), dma((5,))],
        name="finish",
    )(pair, lg, rg, wg, bg)
    return (
        pair.reshape(tile_rows, tile_cols, pair_width),
        lg.reshape(li, width, samples).transpose(2, 0, 1),
        rg.reshape(rj, width, samples).transpose(2, 0, 1),
        wg,
        bg.reshape(pair_width),
    )


def solution(mesh):
    nrow, ncol = mesh.shape["row"], mesh.shape["col"]
    in_specs = (
        P(None, ("row", "col"), None),
        P(None, ("col", "row"), None),
        P(),
        P(),
        P("row", "col", None),
    )
    out_specs = (
        P("row", "col", None),
        P(None, ("row", "col"), None),
        P(None, ("col", "row"), None),
        P(),
        P(),
    )
    return jax.shard_map(
        functools.partial(per_device, nrow, ncol),
        mesh=mesh, in_specs=in_specs, out_specs=out_specs, check_vma=False,
    )
```

profile of v0, /device:TPU:0, one launch (start us, length us, event | category | flops | bytes accessed | tf_op | source)
XLA Modules:
  0.0 50.8 jit_solution(1193147472264510408)
XLA Ops:
  0.6 47.5 %tile.1 = (f32[1024,128]{1,0:T(8,128)}, f32[256,128]{1,0:T(8,128)}, f32[128,128]{1,0:T(8,128)}, f32[8,4,32,128]{3,2,1,0:T(8,128)}, f32[1,128]{1,0:T(1,128)}) custom-call(f32[256,128]{1,0:T(8,128)} %bitcast.17, f32[128,128]{1,0:T(8,128)} %bitcast.18, f32[1024,128]{1,0:T(8,128)} %w_ref.1, f32[1,128]{1,0:T(1,128)} %bitcast.19, f32[1024,128]{1,0:T(8,128)} %bitcast.16), custom_call_target="tpu_custom_call" | custom-call | tf_op jit(solution)/shard_map/tile/pallas_call | solution.py:328
  48.2 2.6 %finish.1 = (f32[1024,128]{1,0:T(8,128)}, f32[256,128]{1,0:T(8,128)}, f32[128,128]{1,0:T(8,128)}, f32[1024,128]{1,0:T(8,128)}, f32[1,128]{1,0:T(1,128)}) custom-call(f32[1024,128]{1,0:T(8,128)} %get-tuple-element.15.pair_ref, f32[256,128]{1,0:T(8,128)} %get-tuple-element.16.lg_ref, f32[128,128]{1,0:T(8,128)} %get-tuple-element.17.rg_ref, ...), custom_call_target="tpu_custom_call" | custom-call | tf_op jit(solution)/shard_map/finish/pallas_call | solution.py:347
where the time goes:
time: 51 us; the launch traced here: 50.8 us
  Pallas kernels  50.2 us (98%)
  between operations  0.64 us (1%)
    pallas_call x1, Pallas kernels, per_device(): pl.pallas_call(functools.partial(tile_kernel, nrow, ncol, width), out_sha...  47.5 us
    pallas_call x1, Pallas kernels, per_device(): pl.pallas_call(functools.partial(finish_kernel, width), out_shape=(shape(...  2.61 us

commit v1 on v0

v1 whole, which is shorter than its diff:
```python
import functools

import jax
import jax.numpy as jnp
from jax import lax
from jax.experimental import pallas as pl
from jax.experimental.pallas import tpu as pltpu
from jax.sharding import PartitionSpec as P

F32 = jnp.float32
BF16 = jnp.bfloat16
MESH = pl.DeviceIdType.MESH
VMEM = pl.BlockSpec(memory_space=pltpu.VMEM)
HBM = pl.BlockSpec(memory_space=pltpu.HBM)
STEP = 8


def in_hbm(x):
    return pltpu.with_memory_space_constraint(x, pltpu.HBM)


def split(x):
    high = x.astype(BF16)
    return high, (x - high.astype(F32)).astype(BF16)


def dot(a, b):
    return lax.dot_general(a, b, (((1,), (0,)), ((), ())), preferred_element_type=F32)


def dot_wide(a_high, a_low, b_both):
    half = b_both.shape[1] // 2
    wide = dot(a_high, b_both)
    return wide[:, 0:half] + (wide[:, half:] + dot(a_low, b_both[:, 0:half]))


def dot_tall(a_both, b_high, b_low):
    half = a_both.shape[0] // 2
    tall = dot(a_both, b_high)
    return tall[0:half] + (tall[half:] + dot(a_both[0:half], b_low))


def total(parts):
    return functools.reduce(lambda a, b: a + b, parts)


def swap_groups(pieces):
    lane = lax.broadcasted_iota(jnp.int32, pieces[0].shape, 1)
    low = lane < 64
    even = (lane & 32) == 0

    def far(a, b):
        moved = pltpu.roll(jnp.where(low, b, a), 64, 1)
        return jnp.where(low, a, moved), jnp.where(low, moved, b)

    def near(a, b):
        return (
            jnp.where(even, a, pltpu.roll(b, 32, 1)),
            jnp.where(even, pltpu.roll(a, 96, 1), b),
        )

    p0, p2 = far(pieces[0], pieces[2])
    p1, p3 = far(pieces[1], pieces[3])
    p0, p1 = near(p0, p1)
    p2, p3 = near(p2, p3)
    return p0, p1, p2, p3


def tile_kernel(
    nrow, ncol, width, l_ref, r_ref, w_ref, b_ref, cot_ref,
    pair_ref, lg_ref, rg_ref, wg_ref, bg_ref,
    lo, ro, lp, lbuf, vbuf, rpa, rp, rbuf,
    wp, cbuf, xs, xbuf, zs, zbuf, bsrc, brow, bmid, bcol,
    w_v, b_v, cot_v, tmp, scr_a, scr_b, acc,
    c2, ct2, w_c, wt2, wt_l, h_h, h_l, rt_c, r2, t_h, t_l, l_c, l_l, lt_c,
    loc, gls, glr, grs, grr, gps, ls, lr, rs, rr, brs, brr, bcs, bcr,
    vr, ks, kr, xss, xsr, zss, zsr, azs, azr, axs, axr, acs, acr,
):
    row, col = lax.axis_index("row"), lax.axis_index("col")
    chip, core = row // 2, lax.rem(row, 2)
    mate = row + 1 - 2 * core
    chips = nrow // 2
    lw, samples = l_ref.shape
    rw = r_ref.shape[0]
    tile_rows, tile_cols = ncol * lw // width, nrow * rw // width
    channels, pair_width = w_ref.shape
    rights = tile_cols * width
    scale = 1.0 / samples
    per = 128 // width
    share = channels // (nrow * ncol)
    lanes_step = STEP * width
    gcols = max(1, lanes_step // lw)
    groups = ncol // gcols
    glanes = gcols * lw
    grows = glanes // width * tile_cols
    own_group = col // gcols
    piece = lw // 2
    lower, upper = col, ncol - 1 - col
    both = jnp.minimum(lower, upper)
    longer = jnp.where(lower > upper, -1, 1)
    inner = jnp.logical_and(col > 0, col < ncol - 1)

    def along(k):
        paired = k <= 2 * both
        distance = jnp.where(paired, (k + 1) // 2, k - both)
        side = jnp.where(jnp.logical_and(paired, lax.rem(k, 2) == 0), -longer, longer)
        return col + side * distance

    def group_at(k):
        return along(k) if gcols == 1 else lax.rem(own_group + k, groups)

    def via_end(source, target):
        return jnp.logical_or(
            jnp.logical_and(source == 0, target >= 3),
            jnp.logical_and(source == ncol - 1, target <= ncol - 4),
        )

    def via_here(target):
        return jnp.logical_or(
            jnp.logical_and(col == 1, target >= 3),
            jnp.logical_and(col == ncol - 2, target <= ncol - 4),
        )

    def in_row(peer):
        return {"row": peer, "col": col}

    def in_col(peer):
        return {"row": row, "col": peer}

    def block(ref, index, size):
        return ref.at[pl.ds(pl.multiple_of(index * size, size), size)]

    def each(count, here, act):
        @pl.loop(1, count)
        def _(k):
            act(lax.rem(here + k, count))

    def each_chip(act):
        each(chips, chip, act)

    def send(src, dst, send_sem, recv_sem, device):
        return pltpu.make_async_remote_copy(
            src_ref=src, dst_ref=dst, send_sem=send_sem, recv_sem=recv_sem,
            device_id=device, device_id_type=MESH,
        )

    def part(ref, index, s):
        return ref.at[pl.ds(pl.multiple_of(index * lw + s * piece, piece), piece)]

    def left_own(s, side):
        return send(
            l_ref.at[pl.ds(s * piece, piece)], part(lo, col, s), gls.at[col, s, (side + 1) // 2], glr.at[col, s],
            in_col(col + side),
        )

    def left_on(q, s):
        return send(
            part(lo, q, s), part(lo, q, s), gls.at[q, s, 0], glr.at[q, s],
            in_col(col + jnp.where(q < col, 1, -1)),
        )

    def right_gather(peer, slot):
        return send(r_ref, block(ro, slot, rw), grs.at[peer], grr.at[slot], in_row(peer))

    def right_pass(slot, there):
        return send(block(ro, slot, rw), block(ro, slot, rw), gps.at[slot // 2], grr.at[there], in_row(mate))

    def left_term(peer, slot):
        return send(block(lp, peer, lw), lbuf.at[slot], ls.at[peer], lr.at[slot], in_col(peer))

    def left_via(peer):
        return send(
            block(lp, peer, lw), vbuf.at[peer], ls.at[peer], vr.at[peer], in_col(jnp.where(col == 0, 1, ncol - 2))
        )

    def right_term(peer, slot):
        return send(block(rp, peer, rw), rbuf.at[slot], rs.at[peer], rr.at[slot], in_row(peer))

    def bias_row(peer, slot):
        return send(bsrc, brow.at[slot], brs.at[peer], brr.at[slot], in_row(peer))

    def bias_col(peer, slot):
        return send(bmid, bcol.at[slot], bcs.at[peer], bcr.at[slot], in_col(peer))

    def core_term(q):
        return send(wp.at[1 - core, q], cbuf.at[q], ks.at[q], kr.at[q], in_row(mate))

    def chip_term(q, peer, slot):
        return send(xs.at[q, peer], xbuf.at[q, slot], xss.at[q, peer], xsr.at[q, slot], in_row(2 * peer + core))

    def col_term(peer, slot):
        return send(zs.at[peer], zbuf.at[slot], zss.at[peer], zsr.at[slot], in_col(peer))

    def col_whole(peer, slot):
        piece = wg_ref.at[core, slot, chip]
        return send(piece, piece, azs.at[peer], azr.at[slot], in_col(peer))

    def chip_whole(q, peer, slot):
        piece = wg_ref.at[core, q, slot]
        return send(piece, piece, axs.at[q, peer], axr.at[q, slot], in_row(2 * peer + core))

    def core_whole(half, q):
        piece = wg_ref.at[half, q]
        return send(piece, piece, acs.at[q], acr.at[q], in_row(mate))

    own_left = pl.ds(pl.multiple_of(col * lw, lw), lw)
    own_right = pl.ds(pl.multiple_of(row * rw, rw), rw)
    loads = [
        pltpu.make_async_copy(src, dst, loc.at[k])
        for k, (src, dst) in enumerate([
            (w_ref, w_v), (cot_ref, cot_v), (r_ref, ro.at[own_right]), (l_ref, lo.at[own_left]), (b_ref, b_v),
        ])
    ]
    barrier = pltpu.get_barrier_semaphore()
    each(ncol, col, lambda p: pl.semaphore_signal(
        barrier, inc=1, device_id=in_col(p), device_id_type=MESH))
    each(nrow, row, lambda p: pl.semaphore_signal(
        barrier, inc=1, device_id=in_row(p), device_id_type=MESH))
    for load in loads:
        load.start()
    pl.semaphore_wait(barrier, nrow + ncol - 2)

    def ends(act):
        for s in range(2):
            @pl.when(col < ncol - 1)
            def _():
                act(left_own(s, 1))

            @pl.when(col > 0)
            def _():
                act(left_own(s, -1))

    ends(lambda copy: copy.start())
    each_chip(lambda m: right_gather(2 * m + core, row).start())
    right_gather(mate, row).start()

    loads[0].wait()
    loads[1].wait()
    for d in range(width):
        tmp[d * width : (d + 1) * width, :] = w_v[pl.ds(d, width, stride=width), :]
    weight = tmp[0:channels, :]
    w_c[:, 0:pair_width], w_c[:, pair_width:] = split(weight)
    high, wt_l[...] = split(weight.T * scale)
    wt2[0:pair_width, :] = high
    wt2[pair_width:, :] = high
    cot = cot_v[...]
    c2[:, 0:pair_width], c2[:, pair_width:] = split(cot)
    ct2[0:pair_width, :], ct2[pair_width:, :] = split(cot.T)
    bsrc[...] = jnp.broadcast_to(jnp.sum(cot, axis=0, keepdims=True), (8, pair_width))
    brow[row] = bsrc[...]
    each(nrow, row, lambda p: bias_row(p, row).start())

    scrs = [scr_a, scr_b]
    steps = channels // lanes_step

    def grad_block(b):
        lanes = slice(b * lanes_step, (b + 1) * lanes_step)
        scrs[b % 2][...] = dot(c2[...], wt2[:, lanes]) + dot(c2[:, 0:pair_width], wt_l[:, lanes])

    def grad_swap(b):
        scr = scrs[b % 2]
        for u in range(STEP // per):
            for v in range(tile_rows // per):
                pieces = [
                    scr[(v * per + a) * tile_cols : (v * per + a + 1) * tile_cols, u * 128 : (u + 1) * 128]
                    for a in range(per)
                ]
                for a, piece in enumerate(swap_groups(pieces)):
                    at = (b * STEP + u * per + a) * tile_cols
                    high, low = split(piece)
                    h_h[at : at + tile_cols, v * 128 : (v + 1) * 128] = high
                    h_l[at : at + tile_cols, v * 128 : (v + 1) * 128] = low

    grad_block(0)
    for b in range(steps):
        if b + 1 < steps:
            grad_block(b + 1)
        grad_swap(b)

    def relay(k):
        @pl.when(inner)
        def _():
            q = along(k)
            for s in range(2):
                left_on(q, s).wait_recv()
                left_on(q, s).start()

    def arrive(k):
        @pl.when(jnp.logical_not(inner))
        def _():
            q = along(k)
            for s in range(2):
                left_on(q, s).wait_recv()

    for k in range(1, min(ncol, 3)):
        relay(k)
    each_chip(lambda m: right_gather(2 * m + core, 2 * m + core).wait_recv())
    each_chip(lambda m: right_pass(2 * m + core, 2 * m + core).start())
    loads[2].wait()
    right_gather(mate, mate).wait_recv()
    each_chip(lambda m: right_pass(2 * m + 1 - core, 2 * m + 1 - core).wait_recv())
    for d in range(width):
        tmp[d * tile_cols : (d + 1) * tile_cols, :] = ro[pl.ds(d, tile_cols, stride=width), :]
    right = tmp[0:rights, :]
    rt_c[:, 0:samples], rt_c[:, samples:] = split(right)
    r2[0:samples, :], r2[samples:, :] = split(right.T)

    @pl.loop(0, groups)
    def _(k):
        g = group_at(groups - 1 - k)
        lanes = pl.ds(pl.multiple_of(g * glanes, glanes), glanes)
        lp[lanes, :] = dot_tall(r2[...], h_h[:, lanes], h_l[:, lanes]).T
        for a in range(gcols):
            peer = g * gcols + a

            @pl.when(via_end(col, peer))
            def _():
                left_via(peer).start()

            @pl.when(jnp.logical_not(jnp.logical_or(peer == col, jnp.logical_or(via_end(col, peer), via_here(peer)))))
            def _():
                left_term(peer, col).start()

            @pl.when(via_end(peer, col))
            def _():
                lbuf[peer] = jnp.zeros(lbuf.shape[1:], F32)

    lbuf[col] = lp[own_left, :]
    if ncol > 3:
        @pl.loop(3, ncol)
        def _(k):
            relay(k)

    each(nrow, row, lambda p: bias_row(p, p).wait_recv())
    bmid[...] = total([brow[q] for q in range(nrow)])
    bcol[col] = bmid[...]
    each(ncol, col, lambda p: bias_col(p, col).start())
    loads[3].wait()
    loads[4].wait()
    acc[...] = jnp.zeros_like(acc)
    rpa[...] = jnp.zeros_like(rpa)

    if gcols > 1:
        @pl.loop(1, ncol)
        def _(k):
            arrive(k)

    def outer_weight(g):
        left = lo[pl.ds(pl.multiple_of(g * glanes, glanes), glanes), :]
        lt_c[:, 0:samples], lt_c[:, samples:] = split(left)
        high, l_l[...] = split(left.T * scale)
        l_c[0:samples, :] = high
        l_c[samples:, :] = high
        half = rights // 2
        for s in range(2):
            at = slice(s * half, (s + 1) * half)
            scrs[s][0:half, 0:glanes] = dot(rt_c[at, :], l_c[...]) + dot(rt_c[at, 0:samples], l_l[...])
        for s in range(2):
            for u in range(width // per // 2):
                for v in range(glanes // 128):
                    pieces = [
                        scrs[s][(u * per + a) * tile_cols : (u * per + a + 1) * tile_cols, v * 128 : (v + 1) * 128]
                        for a in range(per)
                    ]
                    lanes = slice((s * (width // per // 2) + u) * 128, (s * (width // per // 2) + u + 1) * 128)
                    for a, piece in enumerate(swap_groups(pieces)):
                        at = (v * per + a) * tile_cols
                        high, low = split(piece)
                        t_h[at : at + tile_cols, lanes] = high
                        t_l[at : at + tile_cols, lanes] = low
        rows = pl.ds(pl.multiple_of(g * grows, grows), grows)
        acc[...] += dot_tall(ct2[:, rows], t_h[...], t_l[...])

    def pair_right(g):
        rows = pl.ds(pl.multiple_of(g * grows, grows), grows)
        lanes = pl.ds(pl.multiple_of(g * glanes, glanes), glanes)
        pair_ref[rows, :] = dot_wide(t_h[...], t_l[...], w_c[...]) + b_v[...]
        rpa[...] += dot_wide(h_h[:, lanes], h_l[:, lanes], lt_c[...])

    @pl.loop(0, groups - 1)
    def _(k):
        g = group_at(k)
        if gcols == 1:
            @pl.when(k > 0)
            def _():
                arrive(k)

        outer_weight(g)
        pair_right(g)

    last = group_at(groups - 1)
    if gcols == 1 and groups > 1:
        arrive(groups - 1)
    outer_weight(last)
    for i in range(channels // 128):
        terms = acc[:, i * 128 : (i + 1) * 128].T
        for n in range(128 // share):
            q, m = divmod((i * 128) // share + n, chips)
            b, q = divmod(q, ncol)
            wp[b, q, m] = terms[n * share : (n + 1) * share, :]

    @pl.loop(0, ncol)
    def _(k):
        core_term(along(ncol - 1 - k)).start()

    pair_right(last)
    for p in range(ncol):
        @pl.when(via_here(p))
        def _():
            left_via(p).wait_recv()
            lp[p * lw : (p + 1) * lw, :] += vbuf[p]
            left_term(p, col).start()

    @pl.loop(0, ncol)
    def _(k):
        q = along(ncol - 1 - k)
        core_term(q).wait_recv()
        xs[q] = wp[core, q] + cbuf[q]
        xbuf[q, chip] = xs[q, chip]
        each_chip(lambda m: chip_term(q, m, chip).start())

    for d in range(width):
        rp[pl.ds(d, tile_cols, stride=width), :] = rpa[d * tile_cols : (d + 1) * tile_cols, :]
    each(nrow, row, lambda p: right_term(p, row).start())
    rbuf[row] = rp[own_right, :]

    @pl.loop(0, ncol)
    def _(k):
        q = along(ncol - 1 - k)
        each_chip(lambda m: chip_term(q, m, m).wait_recv())
        zs[q] = total([xbuf[q, m] for m in range(chips)])

        @pl.when(k < ncol - 1)
        def _():
            col_term(q, col).start()

    zbuf[col] = zs[col]
    each(ncol, col, lambda p: bias_col(p, p).wait_recv())
    bg_ref[...] = total([bcol[q] for q in range(ncol)])[0:1, :] / (tile_rows * nrow)
    def left_terms(p):
        @pl.when(jnp.logical_not(via_end(p, col)))
        def _():
            left_term(p, p).wait_recv()

    each(ncol, col, left_terms)
    lg_ref[...] = total([lbuf[q] for q in range(ncol)])
    each(ncol, col, lambda p: col_term(p, p).wait_recv())
    wg_ref[core, col, chip] = total([zbuf[q] for q in range(ncol)]) / (tile_rows * nrow)

    @pl.loop(1, ncol)
    def _(k):
        col_whole(along(ncol - k), col).start()

    each_chip(lambda m: chip_whole(col, m, chip).start())
    ends(lambda copy: copy.wait_send())

    @pl.when(inner)
    def _():
        @pl.loop(1, ncol)
        def _(k):
            for s in range(2):
                left_on(along(k), s).wait_send()

    each_chip(lambda m: right_gather(2 * m + core, row).wait_send())
    right_gather(mate, row).wait_send()
    each_chip(lambda m: right_pass(2 * m + core, 2 * m + core).wait_send())
    each(nrow, row, lambda p: bias_row(p, row).wait_send())
    each(ncol, col, lambda p: bias_col(p, col).wait_send())
    each(ncol, col, lambda p: left_term(p, col).wait_send())
    each(ncol, col, lambda p: col_term(p, col).wait_send())

    @pl.loop(0, ncol)
    def _(q):
        core_term(q).wait_send()
        each_chip(lambda m: chip_term(q, m, chip).wait_send())

    each(nrow, row, lambda p: right_term(p, row).wait_send())

    @pl.loop(1, ncol)
    def _(k):
        q = along(k)
        col_whole(q, q).wait_recv()
        each_chip(lambda m: chip_whole(q, m, chip).start())

    @pl.loop(0, ncol)
    def _(k):
        q = along(k)
        each_chip(lambda m: chip_whole(q, m, m).wait_recv())
        core_whole(core, q).start()

    each(nrow, row, lambda p: right_term(p, p).wait_recv())
    rg_ref[...] = total([rbuf[q] for q in range(nrow)])
    each(ncol, col, lambda p: col_whole(p, col).wait_send())

    @pl.loop(0, ncol)
    def _(q):
        each_chip(lambda m: chip_whole(q, m, chip).wait_send())
        core_whole(core, q).wait_send()

    @pl.loop(0, ncol)
    def _(q):
        core_whole(1 - core, q).wait_recv()


def finish_kernel(
    width, pair_ref, lg_ref, rg_ref, wg_ref, bg_ref,
    pair_out, lg_out, rg_out, w_out, bg_out, held, sems,
):
    copies = [
        pltpu.make_async_copy(src, dst, sems.at[k])
        for k, (src, dst) in enumerate([
            (pair_ref, pair_out), (lg_ref, lg_out), (rg_ref, rg_out), (bg_ref, bg_out),
        ])
    ]
    for copy in copies:
        copy.start()
    halves, ncol, chips, share, _ = wg_ref.shape
    for s in range(halves * ncol * chips):
        d, c = divmod(s * share, width)
        q, m = divmod(s, chips)
        b, q = divmod(q, ncol)
        held[pl.ds(c * width + d, share, stride=width), :] = wg_ref[b, q, m]
    last = pltpu.make_async_copy(held, w_out, sems.at[4])
    last.start()
    for copy in [*copies, last]:
        copy.wait()


def per_device(nrow, ncol, left_factors, right_factors, weight, bias, cotangent):
    samples, li, width = left_factors.shape
    rj = right_factors.shape[1]
    tile_rows, tile_cols, pair_width = cotangent.shape
    channels = weight.shape[0]
    lw, rw = li * width, rj * width
    lefts, rights = tile_rows * width, tile_cols * width
    pairs = tile_rows * tile_cols
    chips, share = nrow // 2, channels // (nrow * ncol)
    group = max(lw, STEP * width)
    dma = pltpu.SemaphoreType.DMA

    def shape(*dims):
        return jax.ShapeDtypeStruct(dims, F32)

    def half(*dims):
        return pltpu.VMEM(dims, BF16)

    def buf(*dims):
        return pltpu.VMEM(dims, F32)

    scratch = [
        buf(lefts, samples), buf(rights, samples), buf(lefts, samples), *[buf(ncol, lw, samples)] * 2,
        buf(rights, samples), buf(rights, samples), buf(nrow, rw, samples),
        buf(2, ncol, chips, share, pair_width), *[buf(ncol, chips, share, pair_width)] * 3,
        *[buf(ncol, share, pair_width)] * 2,
        buf(8, pair_width), buf(nrow, 8, pair_width), buf(8, pair_width), buf(ncol, 8, pair_width),
        buf(channels, pair_width), buf(1, pair_width), buf(pairs, pair_width),
        buf(max(rights, channels), 128),
        *[buf(max(pairs, rights), max(group, STEP * width))] * 2, buf(pair_width, channels),
        half(pairs, 2 * pair_width), half(2 * pair_width, pairs), half(channels, 2 * pair_width),
        half(2 * pair_width, channels), half(pair_width, channels),
        half(rights, lefts), half(rights, lefts), half(rights, 2 * samples), half(2 * samples, rights),
        *[half(group // width * tile_cols, channels)] * 2,
        half(2 * samples, group), half(samples, group), half(group, 2 * samples),
        dma((5,)), dma((ncol, 2, 2)), dma((ncol, 2)), dma((nrow,)), dma((nrow,)), dma((chips,)),
        dma((ncol,)), dma((ncol,)), dma((nrow,)), dma((nrow,)),
        dma((nrow,)), dma((nrow,)), dma((ncol,)), dma((ncol,)),
        dma((ncol,)), dma((ncol,)), dma((ncol,)), dma((ncol, chips)), dma((ncol, chips)),
        dma((ncol,)), dma((ncol,)), dma((ncol,)), dma((ncol,)),
        dma((ncol, chips)), dma((ncol, chips)), dma((ncol,)), dma((ncol,)),
    ]
    pair, lg, rg, wg, bg = pl.pallas_call(
        functools.partial(tile_kernel, nrow, ncol, width),
        out_shape=(
            shape(pairs, pair_width), shape(lw, samples), shape(rw, samples),
            shape(2, ncol, chips, share, pair_width), shape(1, pair_width),
        ),
        in_specs=[HBM] * 5,
        out_specs=[VMEM] * 5,
        scratch_shapes=scratch,
        compiler_params=pltpu.CompilerParams(
            collective_id=0, has_side_effects=True, vmem_limit_bytes=40 * 2**20
        ),
        name="tile",
    )(
        in_hbm(left_factors.transpose(1, 2, 0).reshape(lw, samples)),
        in_hbm(right_factors.transpose(1, 2, 0).reshape(rw, samples)),
        in_hbm(weight),
        in_hbm(bias.reshape(1, pair_width)),
        in_hbm(cotangent.reshape(pairs, pair_width)),
    )
    pair, lg, rg, wg, bg = pl.pallas_call(
        functools.partial(finish_kernel, width),
        out_shape=(
            shape(pairs, pair_width), shape(lw, samples), shape(rw, samples),
            shape(channels, pair_width), shape(1, pair_width),
        ),
        in_specs=[VMEM] * 5,
        out_specs=[HBM] * 5,
        scratch_shapes=[buf(channels, pair_width), dma((5,))],
        compiler_params=pltpu.CompilerParams(vmem_limit_bytes=8 * 2**20),
        name="finish",
    )(pair, lg, rg, wg, bg)
    return (
        pair.reshape(tile_rows, tile_cols, pair_width),
        lg.reshape(li, width, samples).transpose(2, 0, 1),
        rg.reshape(rj, width, samples).transpose(2, 0, 1),
        wg,
        bg.reshape(pair_width),
    )


def solution(mesh):
    nrow, ncol = mesh.shape["row"], mesh.shape["col"]
    in_specs = (
        P(None, ("row", "col"), None),
        P(None, ("col", "row"), None),
        P(),
        P(),
        P("row", "col", None),
    )
    out_specs = (
        P("row", "col", None),
        P(None, ("row", "col"), None),
        P(None, ("col", "row"), None),
        P(),
        P(),
    )
    return jax.shard_map(
        functools.partial(per_device, nrow, ncol),
        mesh=mesh, in_specs=in_specs, out_specs=out_specs, check_vma=False,
    )
```

time: 51 us -> 42.3 us (0.83)
  Pallas kernels: 50.2 us -> 41.5 us
    pallas_call x1, Pallas kernels: 47.5 us -> 40.2 us  [per_device(): pl.pallas_call(functools.partial(tile_kernel, nrow, ncol, width), out_sha...]
    pallas_call x1, Pallas kernels: 2.61 us -> 1.32 us  [per_device(): pl.pallas_call(functools.partial(finish_kernel, width), out_shape=(shape(...]
where the time goes in v1:
time: 42.3 us; the launch traced here: 42.2 us
  Pallas kernels  41.5 us (98%)
  between operations  0.64 us (2%)
    pallas_call x1, Pallas kernels, per_device(): pl.pallas_call(functools.partial(tile_kernel, nrow, ncol, width), out_sha...  40.2 us
    pallas_call x1, Pallas kernels, per_device(): pl.pallas_call(functools.partial(finish_kernel, width), out_shape=(shape(...  1.32 us

profile of v1, /device:TPU:0, one launch (start us, length us, event | category | flops | bytes accessed | tf_op | source)
XLA Modules:
  0.0 42.2 jit_solution(11808524113594817182)
XLA Ops:
  0.6 40.2 %tile.1 = (f32[1024,128]{1,0:T(8,128)S(1)}, f32[256,128]{1,0:T(8,128)S(1)}, f32[128,128]{1,0:T(8,128)S(1)}, f32[2,4,4,32,128]{4,3,2,1,0:T(8,128)S(1)}, f32[1,128]{1,0:T(1,128)S(1)}) custom-call(f32[256,128]{1,0:T(8,128)} %bitcast.17, f32[128,128]{1,0:T(8,128)} %bitcast.18, f32[1024,128]{1,0:T(8,128)} %w_ref.1, f32[1,128]{1,0:T(1,128)} %bitcast.19, ...), custom_call_target="tpu_custom_call" | custom-call | tf_op jit(solution)/shard_map/tile/pallas_call | solution.py:571
  40.9 1.3 %finish.1 = (f32[1024,128]{1,0:T(8,128)}, f32[256,128]{1,0:T(8,128)}, f32[128,128]{1,0:T(8,128)}, f32[1024,128]{1,0:T(8,128)}, f32[1,128]{1,0:T(1,128)}) custom-call(f32[1024,128]{1,0:T(8,128)S(1)} %get-tuple-element.15.pair_ref, f32[256,128]{1,0:T(8,128)S(1)} %get-tuple-element.16.lg_ref, f32[128,128]{1,0:T(8,128)S(1)} %get-tuple-element.17.rg_ref, ...), custom_call_target="tpu_custom_call" | custom-call | tf_op jit(solution)/shard_map/finish/pallas_call | solution.py:591

commit v2 on v1

--- a/solution.py
+++ b/solution.py
@@ -13,6 +13,11 @@
 VMEM = pl.BlockSpec(memory_space=pltpu.VMEM)
 HBM = pl.BlockSpec(memory_space=pltpu.HBM)
 STEP = 8
+SINGLE = (
+    "left", "relay", "right", "pass", "same", "mate", "passed", "terms", "term", "via", "swap", "swapped",
+    "rterms", "rterm", "brow", "browed", "bcol", "bcoled", "core", "chip", "col", "coled",
+    "allcol", "allchip", "allcore", "done",
+)
 
 
 def in_hbm(x):
@@ -69,12 +74,11 @@
 def tile_kernel(
     nrow, ncol, width, l_ref, r_ref, w_ref, b_ref, cot_ref,
     pair_ref, lg_ref, rg_ref, wg_ref, bg_ref,
-    lo, ro, lp, lbuf, vbuf, rpa, rp, rbuf,
+    lo, ro, lp, lbuf, vbuf, rpa, rp, mbuf, rsum, rbuf,
     wp, cbuf, xs, xbuf, zs, zbuf, bsrc, brow, bmid, bcol,
     w_v, b_v, cot_v, tmp, scr_a, scr_b, acc,
     c2, ct2, w_c, wt2, wt_l, h_h, h_l, rt_c, r2, t_h, t_l, l_c, l_l, lt_c,
-    loc, gls, glr, grs, grr, gps, ls, lr, rs, rr, brs, brr, bcs, bcr,
-    vr, ks, kr, xss, xsr, zss, zsr, azs, azr, axs, axr, acs, acr,
+    loc, one, glr, kr, xsr, azr, axr,
 ):
     row, col = lax.axis_index("row"), lax.axis_index("col")
     chip, core = row // 2, lax.rem(row, 2)
@@ -135,8 +139,14 @@
         def _(k):
             act(lax.rem(here + k, count))
 
+    wide = chips // 2
+    steps_out = sorted(
+        ((a, b) for a in range(wide) for b in range(2) if a + b), key=lambda s: -(min(s[0], wide - s[0]) + s[1])
+    )
+
     def each_chip(act):
-        each(chips, chip, act)
+        for a, b in steps_out:
+            act(lax.rem(chip // 2 + a, wide) * 2 + lax.rem(chip + b, 2))
 
     def send(src, dst, send_sem, recv_sem, device):
         return pltpu.make_async_remote_copy(
@@ -147,95 +157,103 @@
     def part(ref, index, s):
         return ref.at[pl.ds(pl.multiple_of(index * lw + s * piece, piece), piece)]
 
+    def sem(name):
+        return one.at[SINGLE.index(name)]
+
+    def settle(ref, semaphore):
+        send(ref, ref, semaphore, semaphore, in_row(mate)).wait_recv()
+
     def left_own(s, side):
         return send(
-            l_ref.at[pl.ds(s * piece, piece)], part(lo, col, s), gls.at[col, s, (side + 1) // 2], glr.at[col, s],
-            in_col(col + side),
+            part(lo, col, s), part(lo, col, s), sem("left"), glr.at[col, s], in_col(col + side)
         )
 
     def left_on(q, s):
         return send(
-            part(lo, q, s), part(lo, q, s), gls.at[q, s, 0], glr.at[q, s],
-            in_col(col + jnp.where(q < col, 1, -1)),
+            part(lo, q, s), part(lo, q, s), sem("relay"), glr.at[q, s], in_col(col + jnp.where(q < col, 1, -1))
         )
 
-    def right_gather(peer, slot):
-        return send(r_ref, block(ro, slot, rw), grs.at[peer], grr.at[slot], in_row(peer))
-
-    def right_pass(slot, there):
-        return send(block(ro, slot, rw), block(ro, slot, rw), gps.at[slot // 2], grr.at[there], in_row(mate))
-
-    def left_term(peer, slot):
-        return send(block(lp, peer, lw), lbuf.at[slot], ls.at[peer], lr.at[slot], in_col(peer))
+    def right_own(peer, name):
+        return send(block(ro, row, rw), block(ro, row, rw), sem("right"), sem(name), in_row(peer))
+
+    def right_pass(slot):
+        return send(block(ro, slot, rw), block(ro, slot, rw), sem("pass"), sem("passed"), in_row(mate))
+
+    def left_term(peer):
+        return send(block(lp, peer, lw), lbuf.at[col], sem("terms"), sem("term"), in_col(peer))
 
     def left_via(peer):
         return send(
-            block(lp, peer, lw), vbuf.at[peer], ls.at[peer], vr.at[peer], in_col(jnp.where(col == 0, 1, ncol - 2))
+            block(lp, peer, lw), vbuf.at[peer], sem("terms"), sem("via"), in_col(jnp.where(col == 0, 1, ncol - 2))
         )
 
-    def right_term(peer, slot):
-        return send(block(rp, peer, rw), rbuf.at[slot], rs.at[peer], rr.at[slot], in_row(peer))
-
-    def bias_row(peer, slot):
-        return send(bsrc, brow.at[slot], brs.at[peer], brr.at[slot], in_row(peer))
-
-    def bias_col(peer, slot):
-        return send(bmid, bcol.at[slot], bcs.at[peer], bcr.at[slot], in_col(peer))
+    def right_swap(m):
+        return send(block(rp, 2 * m + 1 - core, rw), mbuf.at[m], sem("swap"), sem("swapped"), in_row(mate))
+
+    def right_term(m):
+        return send(rsum.at[m], rbuf.at[chip], sem("rterms"), sem("rterm"), in_row(2 * m + core))
+
+    def bias_row(peer):
+        return send(bsrc, brow.at[row], sem("brow"), sem("browed"), in_row(peer))
+
+    def bias_col(peer):
+        return send(bmid, bcol.at[col], sem("bcol"), sem("bcoled"), in_col(peer))
 
     def core_term(q):
-        return send(wp.at[1 - core, q], cbuf.at[q], ks.at[q], kr.at[q], in_row(mate))
-
-    def chip_term(q, peer, slot):
-        return send(xs.at[q, peer], xbuf.at[q, slot], xss.at[q, peer], xsr.at[q, slot], in_row(2 * peer + core))
-
-    def col_term(peer, slot):
-        return send(zs.at[peer], zbuf.at[slot], zss.at[peer], zsr.at[slot], in_col(peer))
-
-    def col_whole(peer, slot):
-        piece = wg_ref.at[core, slot, chip]
-        return send(piece, piece, azs.at[peer], azr.at[slot], in_col(peer))
-
-    def chip_whole(q, peer, slot):
-        piece = wg_ref.at[core, q, slot]
-        return send(piece, piece, axs.at[q, peer], axr.at[q, slot], in_row(2 * peer + core))
-
-    def core_whole(half, q):
-        piece = wg_ref.at[half, q]
-        return send(piece, piece, acs.at[q], acr.at[q], in_row(mate))
-
+        return send(wp.at[1 - core, q], cbuf.at[q], sem("core"), kr.at[q], in_row(mate))
+
+    def chip_term(q, m):
+        return send(xs.at[q, m], xbuf.at[q, chip], sem("chip"), xsr.at[q], in_row(2 * m + core))
+
+    def col_term(peer):
+        return send(zs.at[peer], zbuf.at[col], sem("col"), sem("coled"), in_col(peer))
+
+    def col_whole(peer):
+        piece = wg_ref.at[core, col, chip]
+        return send(piece, piece, sem("allcol"), azr.at[col], in_col(peer))
+
+    def chip_whole(q, m):
+        piece = wg_ref.at[core, q, chip]
+        return send(piece, piece, sem("allchip"), axr.at[q], in_row(2 * m + core))
+
+    def core_whole(q):
+        piece = wg_ref.at[core, q]
+        return send(piece, piece, sem("allcore"), sem("done"), in_row(mate))
+
+    others = pl.ds(0, chips - 1)
     own_left = pl.ds(pl.multiple_of(col * lw, lw), lw)
     own_right = pl.ds(pl.multiple_of(row * rw, rw), rw)
     loads = [
         pltpu.make_async_copy(src, dst, loc.at[k])
         for k, (src, dst) in enumerate([
-            (w_ref, w_v), (cot_ref, cot_v), (r_ref, ro.at[own_right]), (l_ref, lo.at[own_left]), (b_ref, b_v),
+            (l_ref, lo.at[own_left]), (r_ref, ro.at[own_right]), (w_ref, w_v), (cot_ref, cot_v), (b_ref, b_v),
         ])
     ]
     barrier = pltpu.get_barrier_semaphore()
+    for load in loads:
+        load.start()
     each(ncol, col, lambda p: pl.semaphore_signal(
         barrier, inc=1, device_id=in_col(p), device_id_type=MESH))
     each(nrow, row, lambda p: pl.semaphore_signal(
         barrier, inc=1, device_id=in_row(p), device_id_type=MESH))
-    for load in loads:
-        load.start()
     pl.semaphore_wait(barrier, nrow + ncol - 2)
-
-    def ends(act):
-        for s in range(2):
-            @pl.when(col < ncol - 1)
-            def _():
-                act(left_own(s, 1))
-
-            @pl.when(col > 0)
-            def _():
-                act(left_own(s, -1))
-
-    ends(lambda copy: copy.start())
-    each_chip(lambda m: right_gather(2 * m + core, row).start())
-    right_gather(mate, row).start()
-
     loads[0].wait()
     loads[1].wait()
+
+    for s in range(2):
+        @pl.when(col < ncol - 1)
+        def _():
+            left_own(s, 1).start()
+
+        @pl.when(col > 0)
+        def _():
+            left_own(s, -1).start()
+
+    each_chip(lambda m: right_own(2 * m + core, "same").start())
+    right_own(mate, "mate").start()
+
+    loads[2].wait()
+    loads[3].wait()
     for d in range(width):
         tmp[d * width : (d + 1) * width, :] = w_v[pl.ds(d, width, stride=width), :]
     weight = tmp[0:channels, :]
@@ -248,7 +266,7 @@
     ct2[0:pair_width, :], ct2[pair_width:, :] = split(cot.T)
     bsrc[...] = jnp.broadcast_to(jnp.sum(cot, axis=0, keepdims=True), (8, pair_width))
     brow[row] = bsrc[...]
-    each(nrow, row, lambda p: bias_row(p, row).start())
+    each(nrow, row, lambda p: bias_row(p).start())
 
     scrs = [scr_a, scr_b]
     steps = channels // lanes_step
@@ -271,34 +289,52 @@
                     h_h[at : at + tile_cols, v * 128 : (v + 1) * 128] = high
                     h_l[at : at + tile_cols, v * 128 : (v + 1) * 128] = low
 
+    def relay(k, s):
+        @pl.when(inner)
+        def _():
+            q = along(k)
+            left_on(q, s).wait_recv()
+            left_on(q, s).start()
+
+    def arrive(k):
+        @pl.when(jnp.logical_not(inner))
+        def _():
+            q = along(k)
+            for s in range(2):
+                left_on(q, s).wait_recv()
+
+    near = range(1, min(ncol, 3))
     grad_block(0)
     for b in range(steps):
         if b + 1 < steps:
             grad_block(b + 1)
+        else:
+            for k in near:
+                relay(k, 0)
         grad_swap(b)
-
-    def relay(k):
-        @pl.when(inner)
-        def _():
-            q = along(k)
-            for s in range(2):
-                left_on(q, s).wait_recv()
-                left_on(q, s).start()
-
-    def arrive(k):
-        @pl.when(jnp.logical_not(inner))
-        def _():
-            q = along(k)
-            for s in range(2):
-                left_on(q, s).wait_recv()
-
-    for k in range(1, min(ncol, 3)):
-        relay(k)
-    each_chip(lambda m: right_gather(2 * m + core, 2 * m + core).wait_recv())
-    each_chip(lambda m: right_pass(2 * m + core, 2 * m + core).start())
-    loads[2].wait()
-    right_gather(mate, mate).wait_recv()
-    each_chip(lambda m: right_pass(2 * m + 1 - core, 2 * m + 1 - core).wait_recv())
+    for k in near:
+        relay(k, 1)
+
+    def right_grad(g, first):
+        left = lo[pl.ds(pl.multiple_of(g * glanes, glanes), glanes), :]
+        lt_c[:, 0:samples], lt_c[:, samples:] = split(left)
+        lanes = pl.ds(pl.multiple_of(g * glanes, glanes), glanes)
+        term = dot_wide(h_h[:, lanes], h_l[:, lanes], lt_c[...])
+        if first:
+            rpa[...] = term
+        else:
+            rpa[...] += term
+
+    early = 2 if gcols == 1 and groups > 2 else 0
+    if early:
+        right_grad(group_at(0), True)
+    settle(block(ro, 0, (chips - 1) * rw), sem("same"))
+    each_chip(lambda m: right_pass(2 * m + core).start())
+    if early:
+        arrive(1)
+        right_grad(group_at(1), False)
+    settle(block(ro, 0, rw), sem("mate"))
+    settle(block(ro, 0, (chips - 1) * rw), sem("passed"))
     for d in range(width):
         tmp[d * tile_cols : (d + 1) * tile_cols, :] = ro[pl.ds(d, tile_cols, stride=width), :]
     right = tmp[0:rights, :]
@@ -310,44 +346,43 @@
         g = group_at(groups - 1 - k)
         lanes = pl.ds(pl.multiple_of(g * glanes, glanes), glanes)
         lp[lanes, :] = dot_tall(r2[...], h_h[:, lanes], h_l[:, lanes]).T
-        for a in range(gcols):
-            peer = g * gcols + a
-
-            @pl.when(via_end(col, peer))
-            def _():
-                left_via(peer).start()
-
-            @pl.when(jnp.logical_not(jnp.logical_or(peer == col, jnp.logical_or(via_end(col, peer), via_here(peer)))))
-            def _():
-                left_term(peer, col).start()
-
-            @pl.when(via_end(peer, col))
-            def _():
-                lbuf[peer] = jnp.zeros(lbuf.shape[1:], F32)
-
-    lbuf[col] = lp[own_left, :]
+
     if ncol > 3:
         @pl.loop(3, ncol)
         def _(k):
-            relay(k)
-
-    each(nrow, row, lambda p: bias_row(p, p).wait_recv())
+            relay(k, 0)
+            relay(k, 1)
+
+    @pl.loop(0, ncol - 1)
+    def _(k):
+        peer = along(ncol - 1 - k)
+
+        @pl.when(via_end(col, peer))
+        def _():
+            left_via(peer).start()
+
+        @pl.when(jnp.logical_not(jnp.logical_or(via_end(col, peer), via_here(peer))))
+        def _():
+            left_term(peer).start()
+
+        @pl.when(via_end(peer, col))
+        def _():
+            lbuf[peer] = jnp.zeros(lbuf.shape[1:], F32)
+
+    lbuf[col] = lp[own_left, :]
+    settle(brow.at[pl.ds(0, nrow - 1)], sem("browed"))
     bmid[...] = total([brow[q] for q in range(nrow)])
     bcol[col] = bmid[...]
-    each(ncol, col, lambda p: bias_col(p, col).start())
-    loads[3].wait()
+    each(ncol, col, lambda p: bias_col(p).start())
     loads[4].wait()
-    acc[...] = jnp.zeros_like(acc)
-    rpa[...] = jnp.zeros_like(rpa)
 
     if gcols > 1:
         @pl.loop(1, ncol)
         def _(k):
             arrive(k)
 
-    def outer_weight(g):
+    def outer(g):
         left = lo[pl.ds(pl.multiple_of(g * glanes, glanes), glanes), :]
-        lt_c[:, 0:samples], lt_c[:, samples:] = split(left)
         high, l_l[...] = split(left.T * scale)
         l_c[0:samples, :] = high
         l_c[samples:, :] = high
@@ -368,30 +403,34 @@
                         high, low = split(piece)
                         t_h[at : at + tile_cols, lanes] = high
                         t_l[at : at + tile_cols, lanes] = low
+
+    def weight_grad(g, lanes, first):
         rows = pl.ds(pl.multiple_of(g * grows, grows), grows)
-        acc[...] += dot_tall(ct2[:, rows], t_h[...], t_l[...])
-
-    def pair_right(g):
+        term = dot_tall(ct2[:, rows], t_h[:, lanes], t_l[:, lanes])
+        if first:
+            acc[:, lanes] = term
+        else:
+            acc[:, lanes] += term
+
+    def pair_rows(g):
         rows = pl.ds(pl.multiple_of(g * grows, grows), grows)
-        lanes = pl.ds(pl.multiple_of(g * glanes, glanes), glanes)
         pair_ref[rows, :] = dot_wide(t_h[...], t_l[...], w_c[...]) + b_v[...]
-        rpa[...] += dot_wide(h_h[:, lanes], h_l[:, lanes], lt_c[...])
-
-    @pl.loop(0, groups - 1)
-    def _(k):
+
+    for k in range(groups - 1):
         g = group_at(k)
-        if gcols == 1:
-            @pl.when(k > 0)
-            def _():
-                arrive(k)
-
-        outer_weight(g)
-        pair_right(g)
+        if gcols == 1 and k >= max(1, early):
+            arrive(k)
+        outer(g)
+        weight_grad(g, slice(0, channels), k == 0)
+        pair_rows(g)
+        if k >= early:
+            right_grad(g, k == 0)
 
     last = group_at(groups - 1)
     if gcols == 1 and groups > 1:
         arrive(groups - 1)
-    outer_weight(last)
+    outer(last)
+    weight_grad(last, slice(0, channels), groups == 1)
     for i in range(channels // 128):
         terms = acc[:, i * 128 : (i + 1) * 128].T
         for n in range(128 // share):
@@ -403,13 +442,18 @@
     def _(k):
         core_term(along(ncol - 1 - k)).start()
 
-    pair_right(last)
+    pair_rows(last)
+    right_grad(last, groups == 1)
+    if ncol > 3:
+        @pl.when(jnp.logical_or(col == 1, col == ncol - 2))
+        def _():
+            settle(vbuf.at[pl.ds(0, ncol - 3)], sem("via"))
+
     for p in range(ncol):
         @pl.when(via_here(p))
         def _():
-            left_via(p).wait_recv()
             lp[p * lw : (p + 1) * lw, :] += vbuf[p]
-            left_term(p, col).start()
+            left_term(p).start()
 
     @pl.loop(0, ncol)
     def _(k):
@@ -417,89 +461,86 @@
         core_term(q).wait_recv()
         xs[q] = wp[core, q] + cbuf[q]
         xbuf[q, chip] = xs[q, chip]
-        each_chip(lambda m: chip_term(q, m, chip).start())
+        each_chip(lambda m: chip_term(q, m).start())
 
     for d in range(width):
         rp[pl.ds(d, tile_cols, stride=width), :] = rpa[d * tile_cols : (d + 1) * tile_cols, :]
-    each(nrow, row, lambda p: right_term(p, row).start())
-    rbuf[row] = rp[own_right, :]
-
-    @pl.loop(0, ncol)
+    for m in range(chips):
+        right_swap(m).start()
+    @pl.loop(0, ncol - 1)
     def _(k):
         q = along(ncol - 1 - k)
-        each_chip(lambda m: chip_term(q, m, m).wait_recv())
+        settle(xbuf.at[q, others], xsr.at[q])
         zs[q] = total([xbuf[q, m] for m in range(chips)])
-
-        @pl.when(k < ncol - 1)
-        def _():
-            col_term(q, col).start()
-
-    zbuf[col] = zs[col]
-    each(ncol, col, lambda p: bias_col(p, p).wait_recv())
+        col_term(q).start()
+
+    settle(mbuf, sem("swapped"))
+    for m in range(chips):
+        rsum[m] = rp[pl.ds(pl.multiple_of((2 * m + core) * rw, rw), rw), :] + mbuf[m]
+    each_chip(lambda m: right_term(m).start())
+    rbuf[chip] = rsum[chip]
+    settle(xbuf.at[col, others], xsr.at[col])
+    zbuf[col] = total([xbuf[col, m] for m in range(chips)])
+    settle(bcol.at[pl.ds(0, ncol - 1)], sem("bcoled"))
     bg_ref[...] = total([bcol[q] for q in range(ncol)])[0:1, :] / (tile_rows * nrow)
-    def left_terms(p):
-        @pl.when(jnp.logical_not(via_end(p, col)))
-        def _():
-            left_term(p, p).wait_recv()
-
-    each(ncol, col, left_terms)
+    near_ends = [jnp.logical_and(ncol > 3, col >= 3), jnp.logical_and(ncol > 3, col <= ncol - 4)]
+    absent = near_ends[0].astype(jnp.int32) + near_ends[1].astype(jnp.int32)
+    for n in range(3):
+        if ncol - 1 - n > 0:
+            @pl.when(absent == n)
+            def _():
+                settle(lbuf.at[pl.ds(0, ncol - 1 - n)], sem("term"))
+
     lg_ref[...] = total([lbuf[q] for q in range(ncol)])
-    each(ncol, col, lambda p: col_term(p, p).wait_recv())
+    settle(zbuf.at[pl.ds(0, ncol - 1)], sem("coled"))
     wg_ref[core, col, chip] = total([zbuf[q] for q in range(ncol)]) / (tile_rows * nrow)
 
     @pl.loop(1, ncol)
     def _(k):
-        col_whole(along(ncol - k), col).start()
-
-    each_chip(lambda m: chip_whole(col, m, chip).start())
-    ends(lambda copy: copy.wait_send())
+        col_whole(along(ncol - k)).start()
+
+    each_chip(lambda m: chip_whole(col, m).start())
+    ends = jnp.logical_not(inner)
 
     @pl.when(inner)
     def _():
-        @pl.loop(1, ncol)
-        def _(k):
-            for s in range(2):
-                left_on(along(k), s).wait_send()
-
-    each_chip(lambda m: right_gather(2 * m + core, row).wait_send())
-    right_gather(mate, row).wait_send()
-    each_chip(lambda m: right_pass(2 * m + core, 2 * m + core).wait_send())
-    each(nrow, row, lambda p: bias_row(p, row).wait_send())
-    each(ncol, col, lambda p: bias_col(p, col).wait_send())
-    each(ncol, col, lambda p: left_term(p, col).wait_send())
-    each(ncol, col, lambda p: col_term(p, col).wait_send())
+        settle(lo.at[pl.ds(0, 2 * lw)], sem("left"))
+        settle(lo.at[pl.ds(0, (ncol - 1) * lw)], sem("relay"))
+
+    @pl.when(ends)
+    def _():
+        settle(lo.at[pl.ds(0, lw)], sem("left"))
+
+    settle(ro.at[pl.ds(0, chips * rw)], sem("right"))
+    settle(ro.at[pl.ds(0, (chips - 1) * rw)], sem("pass"))
+    settle(brow.at[pl.ds(0, nrow - 1)], sem("brow"))
+    settle(bcol.at[pl.ds(0, ncol - 1)], sem("bcol"))
+    settle(wp.at[0], sem("core"))
+    settle(xs.at[:, others], sem("chip"))
+    settle(mbuf, sem("swap"))
+
+    @pl.loop(1, ncol)
+    def _(k):
+        q = along(k)
+        piece_in = wg_ref.at[core, q, chip]
+        settle(piece_in, azr.at[q])
+        each_chip(lambda m: chip_whole(q, m).start())
 
     @pl.loop(0, ncol)
-    def _(q):
-        core_term(q).wait_send()
-        each_chip(lambda m: chip_term(q, m, chip).wait_send())
-
-    each(nrow, row, lambda p: right_term(p, row).wait_send())
-
-    @pl.loop(1, ncol)
     def _(k):
         q = along(k)
-        col_whole(q, q).wait_recv()
-        each_chip(lambda m: chip_whole(q, m, chip).start())
-
-    @pl.loop(0, ncol)
-    def _(k):
-        q = along(k)
-        each_chip(lambda m: chip_whole(q, m, m).wait_recv())
-        core_whole(core, q).start()
-
-    each(nrow, row, lambda p: right_term(p, p).wait_recv())
-    rg_ref[...] = total([rbuf[q] for q in range(nrow)])
-    each(ncol, col, lambda p: col_whole(p, col).wait_send())
-
-    @pl.loop(0, ncol)
-    def _(q):
-        each_chip(lambda m: chip_whole(q, m, chip).wait_send())
-        core_whole(core, q).wait_send()
-
-    @pl.loop(0, ncol)
-    def _(q):
-        core_whole(1 - core, q).wait_recv()
+        settle(wg_ref.at[core, q, others], axr.at[q])
+        core_whole(q).start()
+
+    settle(rbuf.at[others], sem("rterm"))
+    rg_ref[...] = total([rbuf[m] for m in range(chips)])
+    settle(lbuf.at[pl.ds(0, ncol - 1)], sem("terms"))
+    settle(rbuf.at[others], sem("rterms"))
+    settle(zs.at[pl.ds(0, ncol - 1)], sem("col"))
+    settle(zs.at[pl.ds(0, ncol - 1)], sem("allcol"))
+    settle(xs.at[:, others], sem("allchip"))
+    settle(wg_ref.at[1 - core], sem("done"))
+    settle(wg_ref.at[core], sem("allcore"))
 
 
 def finish_kernel(
@@ -549,7 +590,7 @@
 
     scratch = [
         buf(lefts, samples), buf(rights, samples), buf(lefts, samples), *[buf(ncol, lw, samples)] * 2,
-        buf(rights, samples), buf(rights, samples), buf(nrow, rw, samples),
+        buf(rights, samples), buf(rights, samples), *[buf(chips, rw, samples)] * 3,
         buf(2, ncol, chips, share, pair_width), *[buf(ncol, chips, share, pair_width)] * 3,
         *[buf(ncol, share, pair_width)] * 2,
         buf(8, pair_width), buf(nrow, 8, pair_width), buf(8, pair_width), buf(ncol, 8, pair_width),
@@ -561,12 +602,8 @@
         half(rights, lefts), half(rights, lefts), half(rights, 2 * samples), half(2 * samples, rights),
         *[half(group // width * tile_cols, channels)] * 2,
         half(2 * samples, group), half(samples, group), half(group, 2 * samples),
-        dma((5,)), dma((ncol, 2, 2)), dma((ncol, 2)), dma((nrow,)), dma((nrow,)), dma((chips,)),
-        dma((ncol,)), dma((ncol,)), dma((nrow,)), dma((nrow,)),
-        dma((nrow,)), dma((nrow,)), dma((ncol,)), dma((ncol,)),
-        dma((ncol,)), dma((ncol,)), dma((ncol,)), dma((ncol, chips)), dma((ncol, chips)),
+        dma((5,)), dma((len(SINGLE),)), dma((ncol, 2)),
         dma((ncol,)), dma((ncol,)), dma((ncol,)), dma((ncol,)),
-        dma((ncol, chips)), dma((ncol, chips)), dma((ncol,)), dma((ncol,)),
     ]
     pair, lg, rg, wg, bg = pl.pallas_call(
         functools.partial(tile_kernel, nrow, ncol, width),

time: 42.3 us -> 39.7 us (0.939)
  Pallas kernels: 41.5 us -> 38.9 us
    pallas_call x1, Pallas kernels: 40.2 us -> 37.6 us  [per_device(): pl.pallas_call(functools.partial(tile_kernel, nrow, ncol, width), out_sha...]
where the time goes in v2:
time: 39.7 us; the launch traced here: 39.6 us
  Pallas kernels  38.9 us (98%)
  between operations  0.64 us (2%)
    pallas_call x1, Pallas kernels, per_device(): pl.pallas_call(functools.partial(tile_kernel, nrow, ncol, width), out_sha...  37.6 us
    pallas_call x1, Pallas kernels, per_device(): pl.pallas_call(functools.partial(finish_kernel, width), out_shape=(shape(...  1.32 us

profile of v2, /device:TPU:0, one launch (start us, length us, event | category | flops | bytes accessed | tf_op | source)
XLA Modules:
  0.0 39.6 jit_solution(4569026141206636488)
XLA Ops:
  0.6 37.6 %tile.1 = (f32[1024,128]{1,0:T(8,128)S(1)}, f32[256,128]{1,0:T(8,128)S(1)}, f32[128,128]{1,0:T(8,128)S(1)}, f32[2,4,4,32,128]{4,3,2,1,0:T(8,128)S(1)}, f32[1,128]{1,0:T(1,128)S(1)}) custom-call(f32[256,128]{1,0:T(8,128)} %bitcast.17, f32[128,128]{1,0:T(8,128)} %bitcast.18, f32[1024,128]{1,0:T(8,128)} %w_ref.1, f32[1,128]{1,0:T(1,128)} %bitcast.19, ...), custom_call_target="tpu_custom_call" | custom-call | tf_op jit(solution)/shard_map/tile/pallas_call | solution.py:608
  38.2 1.3 %finish.1 = (f32[1024,128]{1,0:T(8,128)}, f32[256,128]{1,0:T(8,128)}, f32[128,128]{1,0:T(8,128)}, f32[1024,128]{1,0:T(8,128)}, f32[1,128]{1,0:T(1,128)}) custom-call(f32[1024,128]{1,0:T(8,128)S(1)} %get-tuple-element.15.pair_ref, f32[256,128]{1,0:T(8,128)S(1)} %get-tuple-element.16.lg_ref, f32[128,128]{1,0:T(8,128)S(1)} %get-tuple-element.17.rg_ref, ...), custom_call_target="tpu_custom_call" | custom-call | tf_op jit(solution)/shard_map/finish/pallas_call | solution.py:628

commit v3 on v2

--- a/solution.py
+++ b/solution.py
@@ -14,8 +14,8 @@
 HBM = pl.BlockSpec(memory_space=pltpu.HBM)
 STEP = 8
 SINGLE = (
-    "left", "relay", "right", "pass", "same", "mate", "passed", "terms", "term", "via", "swap", "swapped",
-    "rterms", "rterm", "brow", "browed", "bcol", "bcoled", "core", "chip", "col", "coled",
+    "left", "relay", "right", "pass", "mate", "passed", "terms", "term", "via", "swap", "swapped",
+    "rterms", "rterm", "bmate", "bmated", "bchip", "bchiped", "bcol", "bcoled", "core", "chip", "col", "coled",
     "allcol", "allchip", "allcore", "done",
 )
 
@@ -75,10 +75,10 @@
     nrow, ncol, width, l_ref, r_ref, w_ref, b_ref, cot_ref,
     pair_ref, lg_ref, rg_ref, wg_ref, bg_ref,
     lo, ro, lp, lbuf, vbuf, rpa, rp, mbuf, rsum, rbuf,
-    wp, cbuf, xs, xbuf, zs, zbuf, bsrc, brow, bmid, bcol,
+    wp, cbuf, xs, xbuf, zs, zbuf, bown, bmate, bsrc, brow, bmid, bcol,
     w_v, b_v, cot_v, tmp, scr_a, scr_b, acc,
     c2, ct2, w_c, wt2, wt_l, h_h, h_l, rt_c, r2, t_h, t_l, l_c, l_l, lt_c,
-    loc, one, glr, kr, xsr, azr, axr,
+    loc, one, glr, grr, kr, xsr, azr, axr,
 ):
     row, col = lax.axis_index("row"), lax.axis_index("col")
     chip, core = row // 2, lax.rem(row, 2)
@@ -102,6 +102,8 @@
     lower, upper = col, ncol - 1 - col
     both = jnp.minimum(lower, upper)
     longer = jnp.where(lower > upper, -1, 1)
+    halfway = ncol // 2
+    low_half = col < halfway
     inner = jnp.logical_and(col > 0, col < ncol - 1)
 
     def along(k):
@@ -110,6 +112,12 @@
         side = jnp.where(jnp.logical_and(paired, lax.rem(k, 2) == 0), -longer, longer)
         return col + side * distance
 
+    def order(k):
+        far = jnp.where(low_half, ncol - 1 - k, k)
+        base = jnp.where(low_half, 0, halfway)
+        near = base + lax.rem(col - base + 1 + lax.rem(k, halfway), halfway)
+        return jnp.where(k < halfway, far, near)
+
     def group_at(k):
         return along(k) if gcols == 1 else lax.rem(own_group + k, groups)
 
@@ -173,8 +181,8 @@
             part(lo, q, s), part(lo, q, s), sem("relay"), glr.at[q, s], in_col(col + jnp.where(q < col, 1, -1))
         )
 
-    def right_own(peer, name):
-        return send(block(ro, row, rw), block(ro, row, rw), sem("right"), sem(name), in_row(peer))
+    def right_own(peer, recv):
+        return send(block(ro, row, rw), block(ro, row, rw), sem("right"), recv, in_row(peer))
 
     def right_pass(slot):
         return send(block(ro, slot, rw), block(ro, slot, rw), sem("pass"), sem("passed"), in_row(mate))
@@ -193,8 +201,11 @@
     def right_term(m):
         return send(rsum.at[m], rbuf.at[chip], sem("rterms"), sem("rterm"), in_row(2 * m + core))
 
-    def bias_row(peer):
-        return send(bsrc, brow.at[row], sem("brow"), sem("browed"), in_row(peer))
+    def bias_mate():
+        return send(bown, bmate, sem("bmate"), sem("bmated"), in_row(mate))
+
+    def bias_chip(m):
+        return send(bsrc, brow.at[chip], sem("bchip"), sem("bchiped"), in_row(2 * m + core))
 
     def bias_col(peer):
         return send(bmid, bcol.at[col], sem("bcol"), sem("bcoled"), in_col(peer))
@@ -232,11 +243,14 @@
     barrier = pltpu.get_barrier_semaphore()
     for load in loads:
         load.start()
-    each(ncol, col, lambda p: pl.semaphore_signal(
-        barrier, inc=1, device_id=in_col(p), device_id_type=MESH))
-    each(nrow, row, lambda p: pl.semaphore_signal(
-        barrier, inc=1, device_id=in_row(p), device_id_type=MESH))
-    pl.semaphore_wait(barrier, nrow + ncol - 2)
+    def hello(device):
+        pl.semaphore_signal(barrier, inc=1, device_id=device, device_id_type=MESH)
+
+    for k in range(1, ncol):
+        hello(in_col(lax.rem(col + k, ncol)))
+    each_chip(lambda m: hello(in_row(2 * m + core)))
+    hello(in_row(mate))
+    pl.semaphore_wait(barrier, ncol + chips - 1)
     loads[0].wait()
     loads[1].wait()
 
@@ -249,8 +263,8 @@
         def _():
             left_own(s, -1).start()
 
-    each_chip(lambda m: right_own(2 * m + core, "same").start())
-    right_own(mate, "mate").start()
+    each_chip(lambda m: right_own(2 * m + core, grr.at[chip]).start())
+    right_own(mate, sem("mate")).start()
 
     loads[2].wait()
     loads[3].wait()
@@ -264,9 +278,8 @@
     cot = cot_v[...]
     c2[:, 0:pair_width], c2[:, pair_width:] = split(cot)
     ct2[0:pair_width, :], ct2[pair_width:, :] = split(cot.T)
-    bsrc[...] = jnp.broadcast_to(jnp.sum(cot, axis=0, keepdims=True), (8, pair_width))
-    brow[row] = bsrc[...]
-    each(nrow, row, lambda p: bias_row(p).start())
+    bown[...] = jnp.broadcast_to(jnp.sum(cot, axis=0, keepdims=True), (8, pair_width))
+    bias_mate().start()
 
     scrs = [scr_a, scr_b]
     steps = channels // lanes_step
@@ -308,12 +321,9 @@
     for b in range(steps):
         if b + 1 < steps:
             grad_block(b + 1)
-        else:
-            for k in near:
-                relay(k, 0)
         grad_swap(b)
     for k in near:
-        relay(k, 1)
+        relay(k, 0)
 
     def right_grad(g, first):
         left = lo[pl.ds(pl.multiple_of(g * glanes, glanes), glanes), :]
@@ -328,8 +338,19 @@
     early = 2 if gcols == 1 and groups > 2 else 0
     if early:
         right_grad(group_at(0), True)
-    settle(block(ro, 0, (chips - 1) * rw), sem("same"))
-    each_chip(lambda m: right_pass(2 * m + core).start())
+    for k in near:
+        relay(k, 1)
+    settle(bmate, sem("bmated"))
+    bsrc[...] = bown[...] + bmate[...]
+    brow[chip] = bsrc[...]
+    each_chip(lambda m: bias_chip(m).start())
+
+    def hand_over(m):
+        settle(block(ro, 0, rw), grr.at[m])
+        right_pass(2 * m + core).start()
+
+    for a, b in reversed(steps_out):
+        hand_over(lax.rem(chip // 2 + a, wide) * 2 + lax.rem(chip + b, 2))
     if early:
         arrive(1)
         right_grad(group_at(1), False)
@@ -341,17 +362,29 @@
     rt_c[:, 0:samples], rt_c[:, samples:] = split(right)
     r2[0:samples, :], r2[samples:, :] = split(right.T)
 
-    @pl.loop(0, groups)
-    def _(k):
+    def left_grad(k):
         g = group_at(groups - 1 - k)
         lanes = pl.ds(pl.multiple_of(g * glanes, glanes), glanes)
         lp[lanes, :] = dot_tall(r2[...], h_h[:, lanes], h_l[:, lanes]).T
 
-    if ncol > 3:
-        @pl.loop(3, ncol)
-        def _(k):
-            relay(k, 0)
-            relay(k, 1)
+    def far_relay(s):
+        if ncol > 3:
+            @pl.loop(3, ncol)
+            def _(k):
+                relay(k, s)
+
+    half = groups // 2
+
+    @pl.loop(0, half)
+    def _(k):
+        left_grad(k)
+
+    far_relay(0)
+    @pl.loop(half, groups)
+    def _(k):
+        left_grad(k)
+
+    far_relay(1)
 
     @pl.loop(0, ncol - 1)
     def _(k):
@@ -370,8 +403,8 @@
             lbuf[peer] = jnp.zeros(lbuf.shape[1:], F32)
 
     lbuf[col] = lp[own_left, :]
-    settle(brow.at[pl.ds(0, nrow - 1)], sem("browed"))
-    bmid[...] = total([brow[q] for q in range(nrow)])
+    settle(brow.at[others], sem("bchiped"))
+    bmid[...] = total([brow[m] for m in range(chips)])
     bcol[col] = bmid[...]
     each(ncol, col, lambda p: bias_col(p).start())
     loads[4].wait()
@@ -381,69 +414,77 @@
         def _(k):
             arrive(k)
 
-    def outer(g):
+    middle = channels // 2
+
+    def outer(g, halves, then):
         left = lo[pl.ds(pl.multiple_of(g * glanes, glanes), glanes), :]
         high, l_l[...] = split(left.T * scale)
         l_c[0:samples, :] = high
         l_c[samples:, :] = high
         half = rights // 2
-        for s in range(2):
-            at = slice(s * half, (s + 1) * half)
-            scrs[s][0:half, 0:glanes] = dot(rt_c[at, :], l_c[...]) + dot(rt_c[at, 0:samples], l_l[...])
-        for s in range(2):
-            for u in range(width // per // 2):
+        units = width // per // 2
+        for scr, h in zip(scrs, halves):
+            at = pl.ds(pl.multiple_of(h * half, half), half)
+            scr[0:half, 0:glanes] = dot(rt_c[at, :], l_c[...]) + dot(rt_c[at, 0:samples], l_l[...])
+        for scr, h in zip(scrs, halves):
+            for u in range(units):
                 for v in range(glanes // 128):
                     pieces = [
-                        scrs[s][(u * per + a) * tile_cols : (u * per + a + 1) * tile_cols, v * 128 : (v + 1) * 128]
+                        scr[(u * per + a) * tile_cols : (u * per + a + 1) * tile_cols, v * 128 : (v + 1) * 128]
                         for a in range(per)
                     ]
-                    lanes = slice((s * (width // per // 2) + u) * 128, (s * (width // per // 2) + u + 1) * 128)
+                    lanes = pl.ds(pl.multiple_of(h * middle + u * 128, 128), 128)
                     for a, piece in enumerate(swap_groups(pieces)):
                         at = (v * per + a) * tile_cols
                         high, low = split(piece)
-                        t_h[at : at + tile_cols, lanes] = high
-                        t_l[at : at + tile_cols, lanes] = low
+                        rows = pl.ds(pl.multiple_of(g * grows + at, tile_cols), tile_cols)
+                        t_h[rows, lanes] = high
+                        t_l[rows, lanes] = low
+            then(h)
 
     def weight_grad(g, lanes, first):
         rows = pl.ds(pl.multiple_of(g * grows, grows), grows)
-        term = dot_tall(ct2[:, rows], t_h[:, lanes], t_l[:, lanes])
+        term = dot_tall(ct2[:, rows], t_h[rows, lanes], t_l[rows, lanes])
         if first:
             acc[:, lanes] = term
         else:
             acc[:, lanes] += term
 
-    def pair_rows(g):
-        rows = pl.ds(pl.multiple_of(g * grows, grows), grows)
-        pair_ref[rows, :] = dot_wide(t_h[...], t_l[...], w_c[...]) + b_v[...]
-
     for k in range(groups - 1):
         g = group_at(k)
         if gcols == 1 and k >= max(1, early):
             arrive(k)
-        outer(g)
+        outer(g, (0, 1), lambda h: None)
         weight_grad(g, slice(0, channels), k == 0)
-        pair_rows(g)
-        if k >= early:
-            right_grad(g, k == 0)
 
     last = group_at(groups - 1)
     if gcols == 1 and groups > 1:
         arrive(groups - 1)
-    outer(last)
-    weight_grad(last, slice(0, channels), groups == 1)
-    for i in range(channels // 128):
-        terms = acc[:, i * 128 : (i + 1) * 128].T
-        for n in range(128 // share):
-            q, m = divmod((i * 128) // share + n, chips)
-            b, q = divmod(q, ncol)
-            wp[b, q, m] = terms[n * share : (n + 1) * share, :]
-
-    @pl.loop(0, ncol)
-    def _(k):
-        core_term(along(ncol - 1 - k)).start()
-
-    pair_rows(last)
-    right_grad(last, groups == 1)
+    turned = jnp.where(low_half, 1, 0)
+
+    def last_half(h):
+        start = pl.multiple_of(h * middle, middle)
+        weight_grad(last, pl.ds(start, middle), groups == 1)
+        for i in range(middle // 128):
+            terms = acc[:, pl.ds(pl.multiple_of(start + i * 128, 128), 128)].T
+            for n in range(128 // share):
+                b, q = divmod((i * 128) // share + n, halfway * chips)
+                q, m = divmod(q, chips)
+                wp[b, h * halfway + q, m] = terms[n * share : (n + 1) * share, :]
+        for q in range(halfway):
+            core_term(h * halfway + q).start()
+
+    outer(last, (turned, 1 - turned), last_half)
+
+    def chip_terms(first):
+        for k in range(first, first + halfway):
+            q = order(k)
+            core_term(q).wait_recv()
+            xs[q] = wp[core, q] + cbuf[q]
+            xbuf[q, chip] = xs[q, chip]
+            each_chip(lambda m: chip_term(q, m).start())
+
+    chip_terms(0)
     if ncol > 3:
         @pl.when(jnp.logical_or(col == 1, col == ncol - 2))
         def _():
@@ -455,30 +496,25 @@
             lp[p * lw : (p + 1) * lw, :] += vbuf[p]
             left_term(p).start()
 
-    @pl.loop(0, ncol)
-    def _(k):
-        q = along(ncol - 1 - k)
-        core_term(q).wait_recv()
-        xs[q] = wp[core, q] + cbuf[q]
-        xbuf[q, chip] = xs[q, chip]
-        each_chip(lambda m: chip_term(q, m).start())
-
+    for k in range(early, groups):
+        right_grad(group_at(k), k == 0)
+    chip_terms(halfway)
     for d in range(width):
         rp[pl.ds(d, tile_cols, stride=width), :] = rpa[d * tile_cols : (d + 1) * tile_cols, :]
     for m in range(chips):
         right_swap(m).start()
-    @pl.loop(0, ncol - 1)
-    def _(k):
-        q = along(ncol - 1 - k)
-        settle(xbuf.at[q, others], xsr.at[q])
-        zs[q] = total([xbuf[q, m] for m in range(chips)])
-        col_term(q).start()
-
+    pair_ref[...] = dot_wide(t_h[...], t_l[...], w_c[...]) + b_v[...]
     settle(mbuf, sem("swapped"))
     for m in range(chips):
         rsum[m] = rp[pl.ds(pl.multiple_of((2 * m + core) * rw, rw), rw), :] + mbuf[m]
     each_chip(lambda m: right_term(m).start())
     rbuf[chip] = rsum[chip]
+    for k in range(ncol - 1):
+        q = order(k)
+        settle(xbuf.at[q, others], xsr.at[q])
+        zs[q] = total([xbuf[q, m] for m in range(chips)])
+        col_term(q).start()
+
     settle(xbuf.at[col, others], xsr.at[col])
     zbuf[col] = total([xbuf[col, m] for m in range(chips)])
     settle(bcol.at[pl.ds(0, ncol - 1)], sem("bcoled"))
@@ -513,7 +549,8 @@
 
     settle(ro.at[pl.ds(0, chips * rw)], sem("right"))
     settle(ro.at[pl.ds(0, (chips - 1) * rw)], sem("pass"))
-    settle(brow.at[pl.ds(0, nrow - 1)], sem("brow"))
+    settle(bown, sem("bmate"))
+    settle(brow.at[others], sem("bchip"))
     settle(bcol.at[pl.ds(0, ncol - 1)], sem("bcol"))
     settle(wp.at[0], sem("core"))
     settle(xs.at[:, others], sem("chip"))
@@ -545,26 +582,27 @@
 
 def finish_kernel(
     width, pair_ref, lg_ref, rg_ref, wg_ref, bg_ref,
-    pair_out, lg_out, rg_out, w_out, bg_out, held, sems,
+    pair_out, lg_out, rg_out, w_out, bg_out, sems,
 ):
+    halves, ncol, chips, share, _ = wg_ref.shape
     copies = [
         pltpu.make_async_copy(src, dst, sems.at[k])
         for k, (src, dst) in enumerate([
             (pair_ref, pair_out), (lg_ref, lg_out), (rg_ref, rg_out), (bg_ref, bg_out),
         ])
     ]
-    for copy in copies:
-        copy.start()
-    halves, ncol, chips, share, _ = wg_ref.shape
     for s in range(halves * ncol * chips):
         d, c = divmod(s * share, width)
         q, m = divmod(s, chips)
-        b, q = divmod(q, ncol)
-        held[pl.ds(c * width + d, share, stride=width), :] = wg_ref[b, q, m]
-    last = pltpu.make_async_copy(held, w_out, sems.at[4])
-    last.start()
-    for copy in [*copies, last]:
+        h, q = divmod(q, ncol)
+        b, q = divmod(q, ncol // 2)
+        q += h * (ncol // 2)
+        pltpu.make_async_copy(wg_ref.at[b, q, m], w_out.at[pl.ds(c, share), d], sems.at[4]).start()
+    for copy in copies:
+        copy.start()
+    for copy in copies:
         copy.wait()
+    pltpu.make_async_copy(wg_ref, wg_ref, sems.at[4]).wait()
 
 
 def per_device(nrow, ncol, left_factors, right_factors, weight, bias, cotangent):
@@ -593,16 +631,16 @@
         buf(rights, samples), buf(rights, samples), *[buf(chips, rw, samples)] * 3,
         buf(2, ncol, chips, share, pair_width), *[buf(ncol, chips, share, pair_width)] * 3,
         *[buf(ncol, share, pair_width)] * 2,
-        buf(8, pair_width), buf(nrow, 8, pair_width), buf(8, pair_width), buf(ncol, 8, pair_width),
+        *[buf(8, pair_width)] * 3, buf(chips, 8, pair_width), buf(8, pair_width), buf(ncol, 8, pair_width),
         buf(channels, pair_width), buf(1, pair_width), buf(pairs, pair_width),
         buf(max(rights, channels), 128),
         *[buf(max(pairs, rights), max(group, STEP * width))] * 2, buf(pair_width, channels),
         half(pairs, 2 * pair_width), half(2 * pair_width, pairs), half(channels, 2 * pair_width),
         half(2 * pair_width, channels), half(pair_width, channels),
         half(rights, lefts), half(rights, lefts), half(rights, 2 * samples), half(2 * samples, rights),
-        *[half(group // width * tile_cols, channels)] * 2,
+        half(pairs, channels), half(pairs, channels),
         half(2 * samples, group), half(samples, group), half(group, 2 * samples),
-        dma((5,)), dma((len(SINGLE),)), dma((ncol, 2)),
+        dma((5,)), dma((len(SINGLE),)), dma((ncol, 2)), dma((chips,)),
         dma((ncol,)), dma((ncol,)), dma((ncol,)), dma((ncol,)),
     ]
     pair, lg, rg, wg, bg = pl.pallas_call(
@@ -629,11 +667,11 @@
         functools.partial(finish_kernel, width),
         out_shape=(
             shape(pairs, pair_width), shape(lw, samples), shape(rw, samples),
-            shape(channels, pair_width), shape(1, pair_width),
+            shape(width, channels // width, pair_width), shape(1, pair_width),
         ),
         in_specs=[VMEM] * 5,
         out_specs=[HBM] * 5,
-        scratch_shapes=[buf(channels, pair_width), dma((5,))],
+        scratch_shapes=[dma((5,))],
         compiler_params=pltpu.CompilerParams(vmem_limit_bytes=8 * 2**20),
         name="finish",
     )(pair, lg, rg, wg, bg)
@@ -641,7 +679,7 @@
         pair.reshape(tile_rows, tile_cols, pair_width),
         lg.reshape(li, width, samples).transpose(2, 0, 1),
         rg.reshape(rj, width, samples).transpose(2, 0, 1),
-        wg,
+        wg.reshape(channels, pair_width),
         bg.reshape(pair_width),
     )
 

time: 39.7 us -> 38.4 us (0.967)
  Pallas kernels: 38.9 us -> 37.6 us
    pallas_call x1, Pallas kernels: 37.6 us -> 36.5 us  [per_device(): pl.pallas_call(functools.partial(tile_kernel, nrow, ncol, width), out_sha...]
where the time goes in v3:
time: 38.4 us; the launch traced here: 38.2 us
  Pallas kernels  37.6 us (98%)
  between operations  0.64 us (2%)
    pallas_call x1, Pallas kernels, per_device(): pl.pallas_call(functools.partial(tile_kernel, nrow, ncol, width), out_sha...  36.5 us
    pallas_call x1, Pallas kernels, per_device(): pl.pallas_call(functools.partial(finish_kernel, width), out_shape=(shape(...  1.06 us

profile of v3, /device:TPU:0, one launch (start us, length us, event | category | flops | bytes accessed | tf_op | source)
XLA Modules:
  0.0 38.2 jit_solution(3557353712997423814)
XLA Ops:
  0.6 36.5 %tile.1 = (f32[1024,128]{1,0:T(8,128)S(1)}, f32[256,128]{1,0:T(8,128)S(1)}, f32[128,128]{1,0:T(8,128)S(1)}, f32[2,4,4,32,128]{4,3,2,1,0:T(8,128)S(1)}, f32[1,128]{1,0:T(1,128)S(1)}) custom-call(f32[256,128]{1,0:T(8,128)} %bitcast.18, f32[128,128]{1,0:T(8,128)} %bitcast.19, f32[1024,128]{1,0:T(8,128)} %w_ref.1, f32[1,128]{1,0:T(1,128)} %bitcast.20, ...), custom_call_target="tpu_custom_call" | custom-call | tf_op jit(solution)/shard_map/tile/pallas_call | solution.py:646
  37.2 1.1 %finish.1 = (f32[1024,128]{1,0:T(8,128)}, f32[256,128]{1,0:T(8,128)}, f32[128,128]{1,0:T(8,128)}, f32[32,32,128]{2,1,0:T(8,128)}, f32[1,128]{1,0:T(1,128)}) custom-call(f32[1024,128]{1,0:T(8,128)S(1)} %get-tuple-element.15.pair_ref, f32[256,128]{1,0:T(8,128)S(1)} %get-tuple-element.16.lg_ref, f32[128,128]{1,0:T(8,128)S(1)} %get-tuple-element.17.rg_ref, ...), custom_call_target="tpu_custom_call" | custom-call | tf_op jit(solution)/shard_map/finish/pallas_call | solution.py:666

commit v4 on v3

--- a/solution.py
+++ b/solution.py
@@ -14,7 +14,7 @@
 HBM = pl.BlockSpec(memory_space=pltpu.HBM)
 STEP = 8
 SINGLE = (
-    "left", "relay", "right", "pass", "mate", "passed", "terms", "term", "via", "swap", "swapped",
+    "left", "leftfar", "relay", "right", "pass", "mate", "passed", "terms", "term", "via", "swap", "swapped",
     "rterms", "rterm", "bmate", "bmated", "bchip", "bchiped", "bcol", "bcoled", "core", "chip", "col", "coled",
     "allcol", "allchip", "allcore", "done",
 )
@@ -168,6 +168,9 @@
     def sem(name):
         return one.at[SINGLE.index(name)]
 
+    def here(act):
+        pl.when(row >= 0)(act)
+
     def settle(ref, semaphore):
         send(ref, ref, semaphore, semaphore, in_row(mate)).wait_recv()
 
@@ -175,6 +178,12 @@
         return send(
             part(lo, col, s), part(lo, col, s), sem("left"), glr.at[col, s], in_col(col + side)
         )
+
+    def left_far(peer, s):
+        return send(part(lo, col, s), part(lo, col, s), sem("leftfar"), glr.at[col, s], in_col(peer))
+
+    def far_off(peer):
+        return jnp.abs(peer - col) >= 3
 
     def left_on(q, s):
         return send(
@@ -263,8 +272,17 @@
         def _():
             left_own(s, -1).start()
 
-    each_chip(lambda m: right_own(2 * m + core, grr.at[chip]).start())
-    right_own(mate, sem("mate")).start()
+    for peer in range(ncol):
+        @pl.when(far_off(peer))
+        def _():
+            for s in range(2):
+                left_far(peer, s).start()
+
+    @here
+    def _():
+        each_chip(lambda m: right_own(2 * m + core, grr.at[chip]).start())
+        right_own(mate, sem("mate")).start()
+
 
     loads[2].wait()
     loads[3].wait()
@@ -310,7 +328,7 @@
             left_on(q, s).start()
 
     def arrive(k):
-        @pl.when(jnp.logical_not(inner))
+        @pl.when(jnp.logical_or(k > 2, jnp.logical_not(inner)))
         def _():
             q = along(k)
             for s in range(2):
@@ -335,7 +353,7 @@
         else:
             rpa[...] += term
 
-    early = 2 if gcols == 1 and groups > 2 else 0
+    early = 1 if gcols == 1 and groups > 1 else 0
     if early:
         right_grad(group_at(0), True)
     for k in near:
@@ -347,13 +365,13 @@
 
     def hand_over(m):
         settle(block(ro, 0, rw), grr.at[m])
-        right_pass(2 * m + core).start()
+
+        @here
+        def _():
+            right_pass(2 * m + core).start()
 
     for a, b in reversed(steps_out):
         hand_over(lax.rem(chip // 2 + a, wide) * 2 + lax.rem(chip + b, 2))
-    if early:
-        arrive(1)
-        right_grad(group_at(1), False)
     settle(block(ro, 0, rw), sem("mate"))
     settle(block(ro, 0, (chips - 1) * rw), sem("passed"))
     for d in range(width):
@@ -362,32 +380,13 @@
     rt_c[:, 0:samples], rt_c[:, samples:] = split(right)
     r2[0:samples, :], r2[samples:, :] = split(right.T)
 
+
     def left_grad(k):
         g = group_at(groups - 1 - k)
         lanes = pl.ds(pl.multiple_of(g * glanes, glanes), glanes)
         lp[lanes, :] = dot_tall(r2[...], h_h[:, lanes], h_l[:, lanes]).T
 
-    def far_relay(s):
-        if ncol > 3:
-            @pl.loop(3, ncol)
-            def _(k):
-                relay(k, s)
-
-    half = groups // 2
-
-    @pl.loop(0, half)
-    def _(k):
-        left_grad(k)
-
-    far_relay(0)
-    @pl.loop(half, groups)
-    def _(k):
-        left_grad(k)
-
-    far_relay(1)
-
-    @pl.loop(0, ncol - 1)
-    def _(k):
+    def send_term(k):
         peer = along(ncol - 1 - k)
 
         @pl.when(via_end(col, peer))
@@ -401,13 +400,6 @@
         @pl.when(via_end(peer, col))
         def _():
             lbuf[peer] = jnp.zeros(lbuf.shape[1:], F32)
-
-    lbuf[col] = lp[own_left, :]
-    settle(brow.at[others], sem("bchiped"))
-    bmid[...] = total([brow[m] for m in range(chips)])
-    bcol[col] = bmid[...]
-    each(ncol, col, lambda p: bias_col(p).start())
-    loads[4].wait()
 
     if gcols > 1:
         @pl.loop(1, ncol)
@@ -416,7 +408,8 @@
 
     middle = channels // 2
 
-    def outer(g, halves, then):
+    def outer(k, halves, beside, then):
+        g = group_at(k)
         left = lo[pl.ds(pl.multiple_of(g * glanes, glanes), glanes), :]
         high, l_l[...] = split(left.T * scale)
         l_c[0:samples, :] = high
@@ -426,6 +419,7 @@
         for scr, h in zip(scrs, halves):
             at = pl.ds(pl.multiple_of(h * half, half), half)
             scr[0:half, 0:glanes] = dot(rt_c[at, :], l_c[...]) + dot(rt_c[at, 0:samples], l_l[...])
+        beside()
         for scr, h in zip(scrs, halves):
             for u in range(units):
                 for v in range(glanes // 128):
@@ -435,46 +429,62 @@
                     ]
                     lanes = pl.ds(pl.multiple_of(h * middle + u * 128, 128), 128)
                     for a, piece in enumerate(swap_groups(pieces)):
-                        at = (v * per + a) * tile_cols
+                        at = k * grows + (v * per + a) * tile_cols
                         high, low = split(piece)
-                        rows = pl.ds(pl.multiple_of(g * grows + at, tile_cols), tile_cols)
-                        t_h[rows, lanes] = high
-                        t_l[rows, lanes] = low
+                        t_h[at : at + tile_cols, lanes] = high
+                        t_l[at : at + tile_cols, lanes] = low
             then(h)
 
-    def weight_grad(g, lanes, first):
-        rows = pl.ds(pl.multiple_of(g * grows, grows), grows)
-        term = dot_tall(ct2[:, rows], t_h[rows, lanes], t_l[rows, lanes])
-        if first:
+    def weight_grad(k, lanes):
+        at = slice(k * grows, (k + 1) * grows)
+        rows = pl.ds(pl.multiple_of(group_at(k) * grows, grows), grows)
+        term = dot_tall(ct2[:, rows], t_h[at, lanes], t_l[at, lanes])
+        if k == 0:
             acc[:, lanes] = term
         else:
             acc[:, lanes] += term
 
+    def beside(k):
+        if k < groups - 1 or gcols > 1:
+            left_grad(k)
+        if k > 0:
+            weight_grad(k - 1, slice(0, channels))
+
     for k in range(groups - 1):
-        g = group_at(k)
         if gcols == 1 and k >= max(1, early):
             arrive(k)
-        outer(g, (0, 1), lambda h: None)
-        weight_grad(g, slice(0, channels), k == 0)
-
-    last = group_at(groups - 1)
+        outer(k, (0, 1), functools.partial(beside, k), lambda h: None)
+        if gcols == 1:
+            @pl.when(jnp.logical_not(inner))
+            def _():
+                send_term(k)
+
+    if gcols == 1:
+        @pl.when(inner)
+        def _():
+            for k in range(groups - 1):
+                send_term(k)
+
     if gcols == 1 and groups > 1:
         arrive(groups - 1)
     turned = jnp.where(low_half, 1, 0)
 
     def last_half(h):
         start = pl.multiple_of(h * middle, middle)
-        weight_grad(last, pl.ds(start, middle), groups == 1)
+        weight_grad(groups - 1, pl.ds(start, middle))
         for i in range(middle // 128):
             terms = acc[:, pl.ds(pl.multiple_of(start + i * 128, 128), 128)].T
             for n in range(128 // share):
                 b, q = divmod((i * 128) // share + n, halfway * chips)
                 q, m = divmod(q, chips)
                 wp[b, h * halfway + q, m] = terms[n * share : (n + 1) * share, :]
-        for q in range(halfway):
-            core_term(h * halfway + q).start()
-
-    outer(last, (turned, 1 - turned), last_half)
+
+        @here
+        def _():
+            for q in range(halfway):
+                core_term(h * halfway + q).start()
+
+    outer(groups - 1, (turned, 1 - turned), functools.partial(beside, groups - 1), last_half)
 
     def chip_terms(first):
         for k in range(first, first + halfway):
@@ -482,41 +492,120 @@
             core_term(q).wait_recv()
             xs[q] = wp[core, q] + cbuf[q]
             xbuf[q, chip] = xs[q, chip]
-            each_chip(lambda m: chip_term(q, m).start())
-
+
+            @here
+            def _():
+                each_chip(lambda m: chip_term(q, m).start())
+
+    if gcols > 1:
+        for k in range(ncol - 1):
+            send_term(k)
     chip_terms(0)
-    if ncol > 3:
-        @pl.when(jnp.logical_or(col == 1, col == ncol - 2))
-        def _():
-            settle(vbuf.at[pl.ds(0, ncol - 3)], sem("via"))
-
-    for p in range(ncol):
-        @pl.when(via_here(p))
-        def _():
-            lp[p * lw : (p + 1) * lw, :] += vbuf[p]
-            left_term(p).start()
-
-    for k in range(early, groups):
+    for k in range(early, groups - 1):
         right_grad(group_at(k), k == 0)
     chip_terms(halfway)
+    loads[4].wait()
+    if gcols == 1:
+        left_grad(groups - 1)
+    lbuf[col] = lp[own_left, :]
+    right_grad(group_at(groups - 1), groups == 1)
+    settle(brow.at[others], sem("bchiped"))
+    bmid[...] = total([brow[m] for m in range(chips)])
+    bcol[col] = bmid[...]
+    each(ncol, col, lambda p: bias_col(p).start())
+
     for d in range(width):
         rp[pl.ds(d, tile_cols, stride=width), :] = rpa[d * tile_cols : (d + 1) * tile_cols, :]
-    for m in range(chips):
-        right_swap(m).start()
-    pair_ref[...] = dot_wide(t_h[...], t_l[...], w_c[...]) + b_v[...]
+
+    @here
+    def _():
+        for m in range(chips):
+            right_swap(m).start()
+
+    pair = dot_wide(t_h[...], t_l[...], w_c[...]) + b_v[...]
+    for k in range(groups):
+        rows = pl.ds(pl.multiple_of(group_at(k) * grows, grows), grows)
+        pair_ref[rows, :] = pair[k * grows : (k + 1) * grows, :]
     settle(mbuf, sem("swapped"))
     for m in range(chips):
         rsum[m] = rp[pl.ds(pl.multiple_of((2 * m + core) * rw, rw), rw), :] + mbuf[m]
-    each_chip(lambda m: right_term(m).start())
+
+    @here
+    def _():
+        each_chip(lambda m: right_term(m).start())
+
     rbuf[chip] = rsum[chip]
     for k in range(ncol - 1):
         q = order(k)
         settle(xbuf.at[q, others], xsr.at[q])
         zs[q] = total([xbuf[q, m] for m in range(chips)])
-        col_term(q).start()
+
+        @here
+        def _():
+            col_term(q).start()
+
+    if ncol > 3:
+        @pl.when(jnp.logical_or(col == 1, col == ncol - 2))
+        def _():
+            settle(vbuf.at[pl.ds(0, ncol - 3)], sem("via"))
+
+    for p in range(ncol):
+        @pl.when(via_here(p))
+        def _():
+            lp[p * lw : (p + 1) * lw, :] += vbuf[p]
+            left_term(p).start()
 
     settle(xbuf.at[col, others], xsr.at[col])
     zbuf[col] = total([xbuf[col, m] for m in range(chips)])
+    settle(zbuf.at[pl.ds(0, ncol - 1)], sem("coled"))
+    wg_ref[core, col, chip] = total([zbuf[q] for q in range(ncol)]) / (tile_rows * nrow)
+
+    @pl.loop(1, ncol)
+    def _(k):
+        col_whole(along(ncol - k)).start()
+
+    @here
+    def _():
+        each_chip(lambda m: chip_whole(col, m).start())
+
+    ends = jnp.logical_not(inner)
+
+    @pl.when(inner)
+    def _():
+        settle(lo.at[pl.ds(0, 2 * lw)], sem("left"))
+        settle(lo.at[pl.ds(0, 2 * lw)], sem("relay"))
+
+    @pl.when(ends)
+    def _():
+        settle(lo.at[pl.ds(0, lw)], sem("left"))
+
+    for peer in range(ncol):
+        @pl.when(far_off(peer))
+        def _():
+            settle(lo.at[pl.ds(0, lw)], sem("leftfar"))
+
+    settle(ro.at[pl.ds(0, chips * rw)], sem("right"))
+    settle(ro.at[pl.ds(0, (chips - 1) * rw)], sem("pass"))
+    settle(bown, sem("bmate"))
+    settle(brow.at[others], sem("bchip"))
+    settle(bcol.at[pl.ds(0, ncol - 1)], sem("bcol"))
+    settle(wp.at[0], sem("core"))
+    settle(xs.at[:, others], sem("chip"))
+    settle(mbuf, sem("swap"))
+
+    @pl.loop(1, ncol)
+    def _(k):
+        q = along(k)
+        piece_in = wg_ref.at[core, q, chip]
+        settle(piece_in, azr.at[q])
+        each_chip(lambda m: chip_whole(q, m).start())
+
+    @pl.loop(0, ncol)
+    def _(k):
+        q = along(k)
+        settle(wg_ref.at[core, q, others], axr.at[q])
+        core_whole(q).start()
+
     settle(bcol.at[pl.ds(0, ncol - 1)], sem("bcoled"))
     bg_ref[...] = total([bcol[q] for q in range(ncol)])[0:1, :] / (tile_rows * nrow)
     near_ends = [jnp.logical_and(ncol > 3, col >= 3), jnp.logical_and(ncol > 3, col <= ncol - 4)]
@@ -528,47 +617,6 @@
                 settle(lbuf.at[pl.ds(0, ncol - 1 - n)], sem("term"))
 
     lg_ref[...] = total([lbuf[q] for q in range(ncol)])
-    settle(zbuf.at[pl.ds(0, ncol - 1)], sem("coled"))
-    wg_ref[core, col, chip] = total([zbuf[q] for q in range(ncol)]) / (tile_rows * nrow)
-
-    @pl.loop(1, ncol)
-    def _(k):
-        col_whole(along(ncol - k)).start()
-
-    each_chip(lambda m: chip_whole(col, m).start())
-    ends = jnp.logical_not(inner)
-
-    @pl.when(inner)
-    def _():
-        settle(lo.at[pl.ds(0, 2 * lw)], sem("left"))
-        settle(lo.at[pl.ds(0, (ncol - 1) * lw)], sem("relay"))
-
-    @pl.when(ends)
-    def _():
-        settle(lo.at[pl.ds(0, lw)], sem("left"))
-
-    settle(ro.at[pl.ds(0, chips * rw)], sem("right"))
-    settle(ro.at[pl.ds(0, (chips - 1) * rw)], sem("pass"))
-    settle(bown, sem("bmate"))
-    settle(brow.at[others], sem("bchip"))
-    settle(bcol.at[pl.ds(0, ncol - 1)], sem("bcol"))
-    settle(wp.at[0], sem("core"))
-    settle(xs.at[:, others], sem("chip"))
-    settle(mbuf, sem("swap"))
-
-    @pl.loop(1, ncol)
-    def _(k):
-        q = along(k)
-        piece_in = wg_ref.at[core, q, chip]
-        settle(piece_in, azr.at[q])
-        each_chip(lambda m: chip_whole(q, m).start())
-
-    @pl.loop(0, ncol)
-    def _(k):
-        q = along(k)
-        settle(wg_ref.at[core, q, others], axr.at[q])
-        core_whole(q).start()
-
     settle(rbuf.at[others], sem("rterm"))
     rg_ref[...] = total([rbuf[m] for m in range(chips)])
     settle(lbuf.at[pl.ds(0, ncol - 1)], sem("terms"))

time: 38.4 us -> 37.2 us (0.969)
  Pallas kernels: 37.6 us -> 36.4 us
    pallas_call x1, Pallas kernels: 36.5 us -> 35.4 us  [per_device(): pl.pallas_call(functools.partial(tile_kernel, nrow, ncol, width), out_sha...]
where the time goes in v4:
time: 37.2 us; the launch traced here: 37.1 us
  Pallas kernels  36.4 us (98%)
  between operations  0.64 us (2%)
    pallas_call x1, Pallas kernels, per_device(): pl.pallas_call(functools.partial(tile_kernel, nrow, ncol, width), out_sha...  35.4 us
    pallas_call x1, Pallas kernels, per_device(): pl.pallas_call(functools.partial(finish_kernel, width), out_shape=(shape(...  1.06 us

profile of v4, /device:TPU:0, one launch (start us, length us, event | category | flops | bytes accessed | tf_op | source)
XLA Modules:
  0.0 37.1 jit_solution(6389929243614504156)
XLA Ops:
  0.6 35.4 %tile.1 = (f32[1024,128]{1,0:T(8,128)S(1)}, f32[256,128]{1,0:T(8,128)S(1)}, f32[128,128]{1,0:T(8,128)S(1)}, f32[2,4,4,32,128]{4,3,2,1,0:T(8,128)S(1)}, f32[1,128]{1,0:T(1,128)S(1)}) custom-call(f32[256,128]{1,0:T(8,128)} %bitcast.18, f32[128,128]{1,0:T(8,128)} %bitcast.19, f32[1024,128]{1,0:T(8,128)} %w_ref.1, f32[1,128]{1,0:T(1,128)} %bitcast.20, ...), custom_call_target="tpu_custom_call" | custom-call | tf_op jit(solution)/shard_map/tile/pallas_call | solution.py:694
  36.0 1.1 %finish.1 = (f32[1024,128]{1,0:T(8,128)}, f32[256,128]{1,0:T(8,128)}, f32[128,128]{1,0:T(8,128)}, f32[32,32,128]{2,1,0:T(8,128)}, f32[1,128]{1,0:T(1,128)}) custom-call(f32[1024,128]{1,0:T(8,128)S(1)} %get-tuple-element.15.pair_ref, f32[256,128]{1,0:T(8,128)S(1)} %get-tuple-element.16.lg_ref, f32[128,128]{1,0:T(8,128)S(1)} %get-tuple-element.17.rg_ref, ...), custom_call_target="tpu_custom_call" | custom-call | tf_op jit(solution)/shard_map/finish/pallas_call | solution.py:714

commit v5 on v4

--- a/solution.py
+++ b/solution.py
@@ -121,6 +121,21 @@
     def group_at(k):
         return along(k) if gcols == 1 else lax.rem(own_group + k, groups)
 
+    crossed = gcols == 1 and groups >= 4
+    span = glanes // 2
+    deep = grows // 2
+
+    def units(k):
+        if crossed and k >= groups - 2:
+            return [2 * group_at(n) + k - (groups - 2) for n in (groups - 2, groups - 1)]
+        return [2 * group_at(k) + n for n in range(2)]
+
+    def lanes_of(ref, k):
+        return jnp.concatenate([ref[:, pl.ds(pl.multiple_of(n * span, span), span)] for n in units(k)], axis=1)
+
+    def rows_of(ref, k):
+        return jnp.concatenate([ref[pl.ds(pl.multiple_of(n * span, span), span), :] for n in units(k)], axis=0)
+
     def via_end(source, target):
         return jnp.logical_or(
             jnp.logical_and(source == 0, target >= 3),
@@ -327,12 +342,19 @@
             left_on(q, s).wait_recv()
             left_on(q, s).start()
 
-    def arrive(k):
+    def arrive(k, pieces=(0, 1)):
         @pl.when(jnp.logical_or(k > 2, jnp.logical_not(inner)))
         def _():
             q = along(k)
-            for s in range(2):
+            for s in pieces:
                 left_on(q, s).wait_recv()
+
+    def ready(k):
+        if crossed and k >= groups - 2:
+            for n in (groups - 2, groups - 1):
+                arrive(n, (k - (groups - 2),))
+        elif gcols == 1 and k > 0:
+            arrive(k)
 
     near = range(1, min(ncol, 3))
     grad_block(0)
@@ -343,19 +365,17 @@
     for k in near:
         relay(k, 0)
 
-    def right_grad(g, first):
-        left = lo[pl.ds(pl.multiple_of(g * glanes, glanes), glanes), :]
-        lt_c[:, 0:samples], lt_c[:, samples:] = split(left)
-        lanes = pl.ds(pl.multiple_of(g * glanes, glanes), glanes)
-        term = dot_wide(h_h[:, lanes], h_l[:, lanes], lt_c[...])
-        if first:
+    def right_grad(k):
+        lt_c[:, 0:samples], lt_c[:, samples:] = split(rows_of(lo, k))
+        term = dot_wide(lanes_of(h_h, k), lanes_of(h_l, k), lt_c[...])
+        if k == 0:
             rpa[...] = term
         else:
             rpa[...] += term
 
     early = 1 if gcols == 1 and groups > 1 else 0
     if early:
-        right_grad(group_at(0), True)
+        right_grad(0)
     for k in near:
         relay(k, 1)
     settle(bmate, sem("bmated"))
@@ -409,9 +429,7 @@
     middle = channels // 2
 
     def outer(k, halves, beside, then):
-        g = group_at(k)
-        left = lo[pl.ds(pl.multiple_of(g * glanes, glanes), glanes), :]
-        high, l_l[...] = split(left.T * scale)
+        high, l_l[...] = split(rows_of(lo, k).T * scale)
         l_c[0:samples, :] = high
         l_c[samples:, :] = high
         half = rights // 2
@@ -437,8 +455,8 @@
 
     def weight_grad(k, lanes):
         at = slice(k * grows, (k + 1) * grows)
-        rows = pl.ds(pl.multiple_of(group_at(k) * grows, grows), grows)
-        term = dot_tall(ct2[:, rows], t_h[at, lanes], t_l[at, lanes])
+        both = jnp.concatenate([ct2[:, pl.ds(pl.multiple_of(n * deep, deep), deep)] for n in units(k)], axis=1)
+        term = dot_tall(both, t_h[at, lanes], t_l[at, lanes])
         if k == 0:
             acc[:, lanes] = term
         else:
@@ -451,8 +469,7 @@
             weight_grad(k - 1, slice(0, channels))
 
     for k in range(groups - 1):
-        if gcols == 1 and k >= max(1, early):
-            arrive(k)
+        ready(k)
         outer(k, (0, 1), functools.partial(beside, k), lambda h: None)
         if gcols == 1:
             @pl.when(jnp.logical_not(inner))
@@ -465,8 +482,7 @@
             for k in range(groups - 1):
                 send_term(k)
 
-    if gcols == 1 and groups > 1:
-        arrive(groups - 1)
+    ready(groups - 1)
     turned = jnp.where(low_half, 1, 0)
 
     def last_half(h):
@@ -502,13 +518,13 @@
             send_term(k)
     chip_terms(0)
     for k in range(early, groups - 1):
-        right_grad(group_at(k), k == 0)
+        right_grad(k)
     chip_terms(halfway)
     loads[4].wait()
     if gcols == 1:
         left_grad(groups - 1)
     lbuf[col] = lp[own_left, :]
-    right_grad(group_at(groups - 1), groups == 1)
+    right_grad(groups - 1)
     settle(brow.at[others], sem("bchiped"))
     bmid[...] = total([brow[m] for m in range(chips)])
     bcol[col] = bmid[...]
@@ -524,8 +540,9 @@
 
     pair = dot_wide(t_h[...], t_l[...], w_c[...]) + b_v[...]
     for k in range(groups):
-        rows = pl.ds(pl.multiple_of(group_at(k) * grows, grows), grows)
-        pair_ref[rows, :] = pair[k * grows : (k + 1) * grows, :]
+        for n, unit in enumerate(units(k)):
+            at = k * grows + n * deep
+            pair_ref[pl.ds(pl.multiple_of(unit * deep, deep), deep), :] = pair[at : at + deep, :]
     settle(mbuf, sem("swapped"))
     for m in range(chips):
         rsum[m] = rp[pl.ds(pl.multiple_of((2 * m + core) * rw, rw), rw), :] + mbuf[m]
@@ -544,17 +561,6 @@
         def _():
             col_term(q).start()
 
-    if ncol > 3:
-        @pl.when(jnp.logical_or(col == 1, col == ncol - 2))
-        def _():
-            settle(vbuf.at[pl.ds(0, ncol - 3)], sem("via"))
-
-    for p in range(ncol):
-        @pl.when(via_here(p))
-        def _():
-            lp[p * lw : (p + 1) * lw, :] += vbuf[p]
-            left_term(p).start()
-
     settle(xbuf.at[col, others], xsr.at[col])
     zbuf[col] = total([xbuf[col, m] for m in range(chips)])
     settle(zbuf.at[pl.ds(0, ncol - 1)], sem("coled"))
@@ -567,6 +573,17 @@
     @here
     def _():
         each_chip(lambda m: chip_whole(col, m).start())
+
+    if ncol > 3:
+        @pl.when(jnp.logical_or(col == 1, col == ncol - 2))
+        def _():
+            settle(vbuf.at[pl.ds(0, ncol - 3)], sem("via"))
+
+    for p in range(ncol):
+        @pl.when(via_here(p))
+        def _():
+            lp[p * lw : (p + 1) * lw, :] += vbuf[p]
+            left_term(p).start()
 
     ends = jnp.logical_not(inner)
 

time: 37.2 us -> 36.4 us (0.978)
  Pallas kernels: 36.4 us -> 35.6 us
    pallas_call x1, Pallas kernels: 35.4 us -> 34.5 us  [per_device(): pl.pallas_call(functools.partial(tile_kernel, nrow, ncol, width), out_sha...]
where the time goes in v5:
time: 36.4 us; the launch traced here: 36.2 us
  Pallas kernels  35.6 us (98%)
  between operations  0.64 us (2%)
    pallas_call x1, Pallas kernels, per_device(): pl.pallas_call(functools.partial(tile_kernel, nrow, ncol, width), out_sha...  34.5 us
    pallas_call x1, Pallas kernels, per_device(): pl.pallas_call(functools.partial(finish_kernel, width), out_shape=(shape(...  1.06 us

profile of v5, /device:TPU:0, one launch (start us, length us, event | category | flops | bytes accessed | tf_op | source)
XLA Modules:
  0.0 36.2 jit_solution(15280228258442929908)
XLA Ops:
  0.6 34.5 %tile.1 = (f32[1024,128]{1,0:T(8,128)S(1)}, f32[256,128]{1,0:T(8,128)S(1)}, f32[128,128]{1,0:T(8,128)S(1)}, f32[2,4,4,32,128]{4,3,2,1,0:T(8,128)S(1)}, f32[1,128]{1,0:T(1,128)S(1)}) custom-call(f32[256,128]{1,0:T(8,128)} %bitcast.18, f32[128,128]{1,0:T(8,128)} %bitcast.19, f32[1024,128]{1,0:T(8,128)} %w_ref.1, f32[1,128]{1,0:T(1,128)} %bitcast.20, ...), custom_call_target="tpu_custom_call" | custom-call | tf_op jit(solution)/shard_map/tile/pallas_call | solution.py:711
  35.2 1.1 %finish.1 = (f32[1024,128]{1,0:T(8,128)}, f32[256,128]{1,0:T(8,128)}, f32[128,128]{1,0:T(8,128)}, f32[32,32,128]{2,1,0:T(8,128)}, f32[1,128]{1,0:T(1,128)}) custom-call(f32[1024,128]{1,0:T(8,128)S(1)} %get-tuple-element.15.pair_ref, f32[256,128]{1,0:T(8,128)S(1)} %get-tuple-element.16.lg_ref, f32[128,128]{1,0:T(8,128)S(1)} %get-tuple-element.17.rg_ref, ...), custom_call_target="tpu_custom_call" | custom-call | tf_op jit(solution)/shard_map/finish/pallas_call | solution.py:731

commit v6 on v5

--- a/solution.py
+++ b/solution.py
@@ -16,7 +16,7 @@
 SINGLE = (
     "left", "leftfar", "relay", "right", "pass", "mate", "passed", "terms", "term", "via", "swap", "swapped",
     "rterms", "rterm", "bmate", "bmated", "bchip", "bchiped", "bcol", "bcoled", "core", "chip", "col", "coled",
-    "allcol", "allchip", "allcore", "done",
+    "allcol", "allchip", "allcore", "alldirect", "done",
 )
 
 
@@ -255,6 +255,10 @@
         piece = wg_ref.at[core, q]
         return send(piece, piece, sem("allcore"), sem("done"), in_row(mate))
 
+    def direct_whole(q, to):
+        piece = wg_ref.at[core, q, chip]
+        return send(piece, piece, sem("alldirect"), sem("done"), in_row(to))
+
     others = pl.ds(0, chips - 1)
     own_left = pl.ds(pl.multiple_of(col * lw, lw), lw)
     own_right = pl.ds(pl.multiple_of(row * rw, rw), rw)
@@ -517,9 +521,9 @@
         for k in range(ncol - 1):
             send_term(k)
     chip_terms(0)
+    chip_terms(halfway)
     for k in range(early, groups - 1):
         right_grad(k)
-    chip_terms(halfway)
     loads[4].wait()
     if gcols == 1:
         left_grad(groups - 1)
@@ -538,31 +542,31 @@
         for m in range(chips):
             right_swap(m).start()
 
+    for k in range(ncol - 1):
+        q = order(k)
+        settle(xbuf.at[q, others], xsr.at[q])
+        zs[q] = total([xbuf[q, m] for m in range(chips)])
+
+        @here
+        def _():
+            col_term(q).start()
+
+    settle(mbuf, sem("swapped"))
+    for m in range(chips):
+        rsum[m] = rp[pl.ds(pl.multiple_of((2 * m + core) * rw, rw), rw), :] + mbuf[m]
+
+    @here
+    def _():
+        each_chip(lambda m: right_term(m).start())
+
+    rbuf[chip] = rsum[chip]
+    settle(xbuf.at[col, others], xsr.at[col])
+    zbuf[col] = total([xbuf[col, m] for m in range(chips)])
     pair = dot_wide(t_h[...], t_l[...], w_c[...]) + b_v[...]
     for k in range(groups):
         for n, unit in enumerate(units(k)):
             at = k * grows + n * deep
             pair_ref[pl.ds(pl.multiple_of(unit * deep, deep), deep), :] = pair[at : at + deep, :]
-    settle(mbuf, sem("swapped"))
-    for m in range(chips):
-        rsum[m] = rp[pl.ds(pl.multiple_of((2 * m + core) * rw, rw), rw), :] + mbuf[m]
-
-    @here
-    def _():
-        each_chip(lambda m: right_term(m).start())
-
-    rbuf[chip] = rsum[chip]
-    for k in range(ncol - 1):
-        q = order(k)
-        settle(xbuf.at[q, others], xsr.at[q])
-        zs[q] = total([xbuf[q, m] for m in range(chips)])
-
-        @here
-        def _():
-            col_term(q).start()
-
-    settle(xbuf.at[col, others], xsr.at[col])
-    zbuf[col] = total([xbuf[col, m] for m in range(chips)])
     settle(zbuf.at[pl.ds(0, ncol - 1)], sem("coled"))
     wg_ref[core, col, chip] = total([zbuf[q] for q in range(ncol)]) / (tile_rows * nrow)
 
@@ -574,16 +578,21 @@
     def _():
         each_chip(lambda m: chip_whole(col, m).start())
 
-    if ncol > 3:
-        @pl.when(jnp.logical_or(col == 1, col == ncol - 2))
-        def _():
-            settle(vbuf.at[pl.ds(0, ncol - 3)], sem("via"))
-
-    for p in range(ncol):
-        @pl.when(via_here(p))
-        def _():
-            lp[p * lw : (p + 1) * lw, :] += vbuf[p]
-            left_term(p).start()
+    def combine():
+        if ncol > 3:
+            @pl.when(jnp.logical_or(col == 1, col == ncol - 2))
+            def _():
+                settle(vbuf.at[pl.ds(0, ncol - 3)], sem("via"))
+
+        for p in range(ncol):
+            @pl.when(via_here(p))
+            def _():
+                lp[p * lw : (p + 1) * lw, :] += vbuf[p]
+                left_term(p).start()
+
+    @pl.when(core == 0)
+    def _():
+        combine()
 
     ends = jnp.logical_not(inner)
 
@@ -617,12 +626,41 @@
         settle(piece_in, azr.at[q])
         each_chip(lambda m: chip_whole(q, m).start())
 
+    @pl.when(core == 0)
+    def _():
+        q = along(ncol - 1)
+        each_chip(lambda m: direct_whole(q, 2 * m + 1).start())
+        direct_whole(q, mate).start()
+
+    @pl.when(core == 1)
+    def _():
+        combine()
+
     @pl.loop(0, ncol)
     def _(k):
         q = along(k)
         settle(wg_ref.at[core, q, others], axr.at[q])
-        core_whole(q).start()
-
+
+        @pl.when(jnp.logical_or(core == 1, k < ncol - 1))
+        def _():
+            core_whole(q).start()
+
+    settle(rbuf.at[others], sem("rterm"))
+    rg_ref[...] = total([rbuf[m] for m in range(chips)])
+    settle(rbuf.at[others], sem("rterms"))
+    settle(zs.at[pl.ds(0, ncol - 1)], sem("col"))
+    settle(zs.at[pl.ds(0, ncol - 1)], sem("allcol"))
+    settle(xs.at[:, others], sem("allchip"))
+    settle(wg_ref.at[1 - core], sem("done"))
+
+    @pl.when(core == 0)
+    def _():
+        settle(wg_ref.at[core, 0], sem("alldirect"))
+        settle(wg_ref.at[core, pl.ds(0, ncol - 1)], sem("allcore"))
+
+    @pl.when(core == 1)
+    def _():
+        settle(wg_ref.at[core], sem("allcore"))
     settle(bcol.at[pl.ds(0, ncol - 1)], sem("bcoled"))
     bg_ref[...] = total([bcol[q] for q in range(ncol)])[0:1, :] / (tile_rows * nrow)
     near_ends = [jnp.logical_and(ncol > 3, col >= 3), jnp.logical_and(ncol > 3, col <= ncol - 4)]
@@ -634,15 +672,7 @@
                 settle(lbuf.at[pl.ds(0, ncol - 1 - n)], sem("term"))
 
     lg_ref[...] = total([lbuf[q] for q in range(ncol)])
-    settle(rbuf.at[others], sem("rterm"))
-    rg_ref[...] = total([rbuf[m] for m in range(chips)])
     settle(lbuf.at[pl.ds(0, ncol - 1)], sem("terms"))
-    settle(rbuf.at[others], sem("rterms"))
-    settle(zs.at[pl.ds(0, ncol - 1)], sem("col"))
-    settle(zs.at[pl.ds(0, ncol - 1)], sem("allcol"))
-    settle(xs.at[:, others], sem("allchip"))
-    settle(wg_ref.at[1 - core], sem("done"))
-    settle(wg_ref.at[core], sem("allcore"))
 
 
 def finish_kernel(

time: 36.4 us -> 35.6 us (0.978)
  Pallas kernels: 35.6 us -> 34.8 us
    pallas_call x1, Pallas kernels: 34.5 us -> 33.7 us  [per_device(): pl.pallas_call(functools.partial(tile_kernel, nrow, ncol, width), out_sha...]
where the time goes in v6:
time: 35.6 us; the launch traced here: 35.4 us
  Pallas kernels  34.8 us (98%)
  between operations  0.64 us (2%)
    pallas_call x1, Pallas kernels, per_device(): pl.pallas_call(functools.partial(tile_kernel, nrow, ncol, width), out_sha...  33.7 us
    pallas_call x1, Pallas kernels, per_device(): pl.pallas_call(functools.partial(finish_kernel, width), out_shape=(shape(...  1.06 us

profile of v6, /device:TPU:0, one launch (start us, length us, event | category | flops | bytes accessed | tf_op | source)
XLA Modules:
  0.0 35.4 jit_solution(16387466969857092972)
XLA Ops:
  0.6 33.7 %tile.1 = (f32[1024,128]{1,0:T(8,128)S(1)}, f32[256,128]{1,0:T(8,128)S(1)}, f32[128,128]{1,0:T(8,128)S(1)}, f32[2,4,4,32,128]{4,3,2,1,0:T(8,128)S(1)}, f32[1,128]{1,0:T(1,128)S(1)}) custom-call(f32[256,128]{1,0:T(8,128)} %bitcast.18, f32[128,128]{1,0:T(8,128)} %bitcast.19, f32[1024,128]{1,0:T(8,128)} %w_ref.1, f32[1,128]{1,0:T(1,128)} %bitcast.20, ...), custom_call_target="tpu_custom_call" | custom-call | tf_op jit(solution)/shard_map/tile/pallas_call | solution.py:741
  34.4 1.1 %finish.1 = (f32[1024,128]{1,0:T(8,128)}, f32[256,128]{1,0:T(8,128)}, f32[128,128]{1,0:T(8,128)}, f32[32,32,128]{2,1,0:T(8,128)}, f32[1,128]{1,0:T(1,128)}) custom-call(f32[1024,128]{1,0:T(8,128)S(1)} %get-tuple-element.15.pair_ref, f32[256,128]{1,0:T(8,128)S(1)} %get-tuple-element.16.lg_ref, f32[128,128]{1,0:T(8,128)S(1)} %get-tuple-element.17.rg_ref, ...), custom_call_target="tpu_custom_call" | custom-call | tf_op jit(solution)/shard_map/finish/pallas_call | solution.py:761

commit v7 on v6

--- a/solution.py
+++ b/solution.py
@@ -186,6 +186,11 @@
     def here(act):
         pl.when(row >= 0)(act)
 
+    def fence():
+        @pl.when(row < 0)
+        def _():
+            tmp[0:8, :] = jnp.zeros((8, tmp.shape[1]), F32)
+
     def settle(ref, semaphore):
         send(ref, ref, semaphore, semaphore, in_row(mate)).wait_recv()
 
@@ -303,6 +308,8 @@
         right_own(mate, sem("mate")).start()
 
 
+    fence()
+
     loads[2].wait()
     loads[3].wait()
     for d in range(width):
@@ -318,6 +325,8 @@
     bown[...] = jnp.broadcast_to(jnp.sum(cot, axis=0, keepdims=True), (8, pair_width))
     bias_mate().start()
 
+    fence()
+
     scrs = [scr_a, scr_b]
     steps = channels // lanes_step
 
@@ -366,6 +375,8 @@
         if b + 1 < steps:
             grad_block(b + 1)
         grad_swap(b)
+    fence()
+
     for k in near:
         relay(k, 0)
 
@@ -378,10 +389,14 @@
             rpa[...] += term
 
     early = 1 if gcols == 1 and groups > 1 else 0
+    fence()
+
     if early:
         right_grad(0)
     for k in near:
         relay(k, 1)
+    fence()
+
     settle(bmate, sem("bmated"))
     bsrc[...] = bown[...] + bmate[...]
     brow[chip] = bsrc[...]
@@ -398,6 +413,8 @@
         hand_over(lax.rem(chip // 2 + a, wide) * 2 + lax.rem(chip + b, 2))
     settle(block(ro, 0, rw), sem("mate"))
     settle(block(ro, 0, (chips - 1) * rw), sem("passed"))
+    fence()
+
     for d in range(width):
         tmp[d * tile_cols : (d + 1) * tile_cols, :] = ro[pl.ds(d, tile_cols, stride=width), :]
     right = tmp[0:rights, :]

time: 35.6 us -> 35.2 us (0.989)
  Pallas kernels: 34.8 us -> 34.4 us
    pallas_call x1, Pallas kernels: 33.7 us -> 33.3 us  [per_device(): pl.pallas_call(functools.partial(tile_kernel, nrow, ncol, width), out_sha...]
where the time goes in v7:
time: 35.2 us; the launch traced here: 35 us
  Pallas kernels  34.4 us (98%)
  between operations  0.64 us (2%)
    pallas_call x1, Pallas kernels, per_device(): pl.pallas_call(functools.partial(tile_kernel, nrow, ncol, width), out_sha...  33.3 us
    pallas_call x1, Pallas kernels, per_device(): pl.pallas_call(functools.partial(finish_kernel, width), out_shape=(shape(...  1.06 us

profile of v7, /device:TPU:0, one launch (start us, length us, event | category | flops | bytes accessed | tf_op | source)
XLA Modules:
  0.0 35.0 jit_solution(7736558419051672761)
XLA Ops:
  0.6 33.3 %tile.1 = (f32[1024,128]{1,0:T(8,128)S(1)}, f32[256,128]{1,0:T(8,128)S(1)}, f32[128,128]{1,0:T(8,128)S(1)}, f32[2,4,4,32,128]{4,3,2,1,0:T(8,128)S(1)}, f32[1,128]{1,0:T(1,128)S(1)}) custom-call(f32[256,128]{1,0:T(8,128)} %bitcast.18, f32[128,128]{1,0:T(8,128)} %bitcast.19, f32[1024,128]{1,0:T(8,128)} %w_ref.1, f32[1,128]{1,0:T(1,128)} %bitcast.20, ...), custom_call_target="tpu_custom_call" | custom-call | tf_op jit(solution)/shard_map/tile/pallas_call | solution.py:758
  34.0 1.1 %finish.1 = (f32[1024,128]{1,0:T(8,128)}, f32[256,128]{1,0:T(8,128)}, f32[128,128]{1,0:T(8,128)}, f32[32,32,128]{2,1,0:T(8,128)}, f32[1,128]{1,0:T(1,128)}) custom-call(f32[1024,128]{1,0:T(8,128)S(1)} %get-tuple-element.15.pair_ref, f32[256,128]{1,0:T(8,128)S(1)} %get-tuple-element.16.lg_ref, f32[128,128]{1,0:T(8,128)S(1)} %get-tuple-element.17.rg_ref, ...), custom_call_target="tpu_custom_call" | custom-call | tf_op jit(solution)/shard_map/finish/pallas_call | solution.py:778

commit v8 on v7

--- a/solution.py
+++ b/solution.py
@@ -360,7 +360,7 @@
         def _():
             q = along(k)
             for s in pieces:
-                left_on(q, s).wait_recv()
+                settle(part(lo, q, s), glr.at[q, s])
 
     def ready(k):
         if crossed and k >= groups - 2:
@@ -374,11 +374,20 @@
     for b in range(steps):
         if b + 1 < steps:
             grad_block(b + 1)
+        else:
+            @pl.when(core == 1)
+            def _():
+                for k in near:
+                    relay(k, 0)
+
         grad_swap(b)
     fence()
 
-    for k in near:
-        relay(k, 0)
+    @pl.when(core == 0)
+    def _():
+        for k in near:
+            relay(k, 0)
+
 
     def right_grad(k):
         lt_c[:, 0:samples], lt_c[:, samples:] = split(rows_of(lo, k))

time: 35.2 us -> 35.1 us (level)
  no operation moved by 1% of the time
where the time goes in v8:
time: 35.1 us; the launch traced here: 34.9 us
  Pallas kernels  34.3 us (98%)
  between operations  0.64 us (2%)
    pallas_call x1, Pallas kernels, per_device(): pl.pallas_call(functools.partial(tile_kernel, nrow, ncol, width), out_sha...  33.2 us
    pallas_call x1, Pallas kernels, per_device(): pl.pallas_call(functools.partial(finish_kernel, width), out_shape=(shape(...  1.06 us

profile of v8, /device:TPU:0, one launch (start us, length us, event | category | flops | bytes accessed | tf_op | source)
XLA Modules:
  0.0 34.9 jit_solution(9276951448629025877)
XLA Ops:
  0.6 33.2 %tile.1 = (f32[1024,128]{1,0:T(8,128)S(1)}, f32[256,128]{1,0:T(8,128)S(1)}, f32[128,128]{1,0:T(8,128)S(1)}, f32[2,4,4,32,128]{4,3,2,1,0:T(8,128)S(1)}, f32[1,128]{1,0:T(1,128)S(1)}) custom-call(f32[256,128]{1,0:T(8,128)} %bitcast.18, f32[128,128]{1,0:T(8,128)} %bitcast.19, f32[1024,128]{1,0:T(8,128)} %w_ref.1, f32[1,128]{1,0:T(1,128)} %bitcast.20, ...), custom_call_target="tpu_custom_call" | custom-call | tf_op jit(solution)/shard_map/tile/pallas_call | solution.py:767
  33.8 1.1 %finish.1 = (f32[1024,128]{1,0:T(8,128)}, f32[256,128]{1,0:T(8,128)}, f32[128,128]{1,0:T(8,128)}, f32[32,32,128]{2,1,0:T(8,128)}, f32[1,128]{1,0:T(1,128)}) custom-call(f32[1024,128]{1,0:T(8,128)S(1)} %get-tuple-element.15.pair_ref, f32[256,128]{1,0:T(8,128)S(1)} %get-tuple-element.16.lg_ref, f32[128,128]{1,0:T(8,128)S(1)} %get-tuple-element.17.rg_ref, ...), custom_call_target="tpu_custom_call" | custom-call | tf_op jit(solution)/shard_map/finish/pallas_call | solution.py:787
